TPU v7x, 128 devices: a whole 4x4x4 slice. The times are simulated.
128 devices in a mesh: ba: 16 (over y_lo, z, core), ha: 8 (over y_hi, x).
Axes of the slice: x: 4, y: 4 (y_hi: 2, y_lo: 2; y = y_hi * 2 + y_lo), z: 4, core: 2. Of those that a mesh axis runs over, the one named last changes fastest.
Arguments:
- queries: bfloat16 [4096, 64, 576], P('ba', 'ha'), may hold values from -6 to 6
- out_grad: bfloat16 [4096, 64, 512], P('ba', 'ha'), may hold values from -1.1953125 to 1.1953125
- out_saved: bfloat16 [4096, 64, 512], P('ba', 'ha'), may hold values from -3 to 3
- logsumexp: float32 [4096, 64], P('ba', 'ha'), may hold values from 7 to 9
- parents: int32 [4096], P('ba'), may hold values from 0 to 1023, as said below
- latents: bfloat16 [1024, 576], P(('ba', 'ha')), may hold values from -6 to 6
- hidden: bfloat16 [1024, 7168], P('ba', 'ha'), may hold values from -6 to 6
- latent_weight: bfloat16 [576, 7168], P(None, 'ha'), may hold values from -0.0625 to 0.0625
Outputs:
- query_grad: bfloat16 [4096, 64, 576], P('ba', 'ha')
- weight_grad: bfloat16 [576, 7168], P('ba', 'ha')
- input_grad: bfloat16 [1024, 7168], P('ba', 'ha')
Inputs may be any that keep to these rules, and one draw needn't show every extreme that they name: `parents`: the 32 tokens of each aligned block of 32 share one value; some token has 0 and some has 1023.
All inputs are finite; a program needn't handle non-finite values.
Results may differ from a plain program's by a relative error of at most 0.0067.
Values may be sent and summed in bfloat16 or wider, within the bound.
A program may use at most 64 MiB of HBM per device.

v0:
```python
import jax
import jax.numpy as jnp
from jax import lax
from jax.sharding import PartitionSpec as P

RANK = 512
ROPE = 64


softmax_scale = 192.0 ** (-0.5)


def cut_along(shard, dim, peers):
    before, after = (shard.shape[:dim], shard.shape[dim + 1 :])
    return jnp.moveaxis(shard.reshape(*before, peers, -1, *after), dim, 0)


def sent_and_summed(shard, axis, dim):
    peers = lax.axis_size(axis)
    pieces = lax.all_to_all(cut_along(shard, dim, peers), axis, 0, 0, tiled=True)
    return jnp.sum(pieces, axis=0)


def from_everyone(shard, axis):
    peers = lax.axis_size(axis)
    return lax.all_to_all(
        jnp.broadcast_to(shard[None], (peers, *shard.shape)), axis, 0, 0, tiled=True
    )


def over_copies(shard, axis):
    return from_everyone(shard, axis).sum(axis=0)


def tile_terms(query_rows, grad_rows, lse_rows, deltas, limits, key_block, offset):
    key_count = key_block.shape[0]
    key_index = offset + jnp.arange(key_count, dtype=jnp.int32)
    scores = (
        jnp.einsum("qd,kd->qk", query_rows, key_block, preferred_element_type=jnp.float32)
        * softmax_scale
    )
    visible = key_index[None, :] <= limits[:, None]
    weights = jnp.where(visible, jnp.exp(scores - lse_rows[:, None]), jnp.float32(0.0))
    grad_prob = jnp.einsum(
        "qd,kd->qk", grad_rows, key_block[:, :RANK], preferred_element_type=jnp.float32
    )
    grad_score = (weights * (grad_prob - deltas[:, None])).astype(jnp.bfloat16)
    query_part = jnp.einsum("qk,kd->qd", grad_score, key_block, preferred_element_type=jnp.float32)
    value_part = jnp.einsum(
        "qk,qd->kd", weights.astype(jnp.bfloat16), grad_rows, preferred_element_type=jnp.float32
    )
    key_grad = softmax_scale * jnp.einsum(
        "qk,qd->kd", grad_score, query_rows, preferred_element_type=jnp.float32
    )
    key_grad = key_grad + jnp.pad(value_part, ((0, 0), (0, ROPE)))
    return (query_part, key_grad)


def on_device(queries, out_grad, out_saved, logsumexp, parents, latents, hidden, latent_weight):
    tokens_here, heads_here, full_width = queries.shape
    row_total = tokens_here * heads_here
    query_rows = queries.reshape(row_total, full_width)
    grad_rows = out_grad.reshape(row_total, RANK)
    saved_rows = out_saved.reshape(row_total, RANK)
    lse_rows = logsumexp.reshape(row_total)
    limits = jnp.repeat(parents, heads_here)
    deltas = jnp.sum(saved_rows.astype(jnp.float32) * grad_rows.astype(jnp.float32), axis=1)
    all_keys = lax.all_gather(latents, ("ba", "ha"), axis=0, tiled=True)
    prefix_total = all_keys.shape[0]
    tile_len = min(256, prefix_total)
    tile_count = prefix_total // tile_len
    key_tiles = all_keys.reshape(tile_count, tile_len, full_width)
    offsets = jnp.arange(tile_count, dtype=jnp.int32) * tile_len

    def tile_step(query_acc, tile_inputs):
        key_block, offset = tile_inputs
        query_part, key_grad = tile_terms(
            query_rows, grad_rows, lse_rows, deltas, limits, key_block, offset
        )
        return (query_acc + query_part, key_grad)

    query_acc, key_stack = lax.scan(
        tile_step, jnp.zeros((row_total, full_width), jnp.float32), (key_tiles, offsets)
    )
    latent_acc = key_stack.reshape(prefix_total, full_width)
    query_grad = (
        (softmax_scale * query_acc)
        .astype(jnp.bfloat16)
        .reshape(tokens_here, heads_here, full_width)
    )
    branch_part = sent_and_summed(latent_acc, "ba", 0)
    row_grads = over_copies(branch_part, "ha").astype(jnp.bfloat16)
    weight_grad = sent_and_summed(
        jnp.einsum("pl,ph->lh", row_grads, hidden, preferred_element_type=jnp.float32), "ba", 0
    ).astype(jnp.bfloat16)
    input_grad = jnp.dot(row_grads, latent_weight, preferred_element_type=jnp.float32).astype(
        jnp.bfloat16
    )
    return (query_grad, weight_grad, input_grad)


def solution(mesh):
    return jax.shard_map(
        on_device,
        mesh=mesh,
        in_specs=(
            P("ba", "ha", None),
            P("ba", "ha", None),
            P("ba", "ha", None),
            P("ba", "ha"),
            P("ba"),
            P(("ba", "ha"), None),
            P("ba", "ha"),
            P(None, "ha"),
        ),
        out_specs=(P("ba", "ha", None), P("ba", "ha"), P("ba", "ha")),
        check_vma=False,
    )
```

profile of v0, /device:TPU:1, one launch (start us, length us, event | category | flops | bytes accessed | tf_op | source)
XLA Modules:
  0.0 485.4 jit_solution(854251680802731591)
XLA Ops:
  7.2 0.7 all-gather.2.cloned.1.call-update
  7.9 0.8 copy.21
  8.8 0.1 sub.59
  8.9 2.8 multiply_reduce_fusion
  11.9 5.1 %copy.20 = bf16[256,8,576]{2,1,0:T(8,128)(2,1)} copy(bf16[256,8,576]{0,2,1:T(8,128)(2,1)} %param.10) | data formatting | bytes 4718592 | tf_op args[0]
  16.9 298.2 %all-gather.2.cloned.1.call-done = bf16[1024,576]{1,0:T(8,128)(2,1)} async-done(((bf16[8,576]{1,0:T(8,128)(2,1)}), bf16[1024,576]{1,0:T(8,128)(2,1)}) %all-gather.2.cloned.1.call-update) | async-done | bytes 1179664 | tf_op jit(solution)/shard_map/all_gather | solution.py:68
  315.1 55.1 %while.16 = (s32[]{:T(128)}, f32[2048,576]{0,1:T(8,128)}, f32[4,256,576]{1,2,0:T(8,128)}, s32[4]{0:T(128)S(1)}, bf16[4,256,576]{2,1,0:T(8,128)(2,1)}, /*index=5*...) while((s32[]{:T(128)}, f32[2048,576]{0,1:T(8,128)}, ...), condition=%wide.wide.region_2.3_spmd.clone, body=%wide.wide.region_1.2_spmd.clone.sunk | while | flops 2892529920 | bytes 73387280 | solution.py:82
  315.1 0.6 dynamic_slice.22
  315.7 0.6 iota_add_fusion.3
  316.4 0.1 le.46
  316.5 1.0 dynamic-slice_bitcast_fusion.3
  317.6 2.8 fusion.69
  320.4 1.0 fusion.71
  321.4 0.8 fusion.70
  322.2 1.2 copy-done.3
  323.4 2.0 fusion.72
  325.4 1.4 select_add_fusion.3
  326.8 2.1 copy-done.2
  328.9 0.6 dynamic_slice.22
  329.5 0.6 iota_add_fusion.3
  330.2 0.1 le.46
  330.3 1.0 dynamic-slice_bitcast_fusion.3
  331.3 2.8 fusion.69
  334.2 1.0 fusion.71
  335.2 0.7 fusion.70
  335.9 1.2 copy-done.3
  337.2 2.0 fusion.72
  339.1 1.4 select_add_fusion.3
  340.5 2.1 copy-done.2
  342.7 0.6 dynamic_slice.22
  343.3 0.6 iota_add_fusion.3
  344.0 0.1 le.46
  344.1 1.0 dynamic-slice_bitcast_fusion.3
  345.1 2.8 fusion.69
  348.0 1.0 fusion.71
  349.0 0.8 fusion.70
  349.7 1.2 copy-done.3
  351.0 2.0 fusion.72
  352.9 1.4 select_add_fusion.3
  354.3 2.1 copy-done.2
  356.4 0.6 dynamic_slice.22
  357.0 0.6 iota_add_fusion.3
  357.8 0.1 le.46
  357.9 1.0 dynamic-slice_bitcast_fusion.3
  358.9 2.8 fusion.69
  361.8 1.0 fusion.71
  362.8 0.7 fusion.70
  363.5 1.2 copy-done.3
  364.8 2.0 fusion.72
  366.7 1.4 select_add_fusion.3
  368.1 2.1 copy-done.2
  370.2 3.2 copy.23
  373.4 37.6 %all_to_all.15 = f32[16,64,576]{2,1,0:T(8,128)} all-to-all(f32[16,64,576]{2,1,0:T(8,128)} %bitcast.77), channel_id=1, replica_groups=mesh['ba'=16,'ha'=8] {'ba'}, dimensions={0} | all-to-all | bytes 4718592 | tf_op jit(solution)/shard_map/all_to_all | solution.py:20
  411.0 1.9 reduce_sum.40
  413.0 24.6 %all_to_all.16 = f32[8,64,576]{2,1,0:T(8,128)S(1)} all-to-all(f32[8,64,576]{2,1,0:T(8,128)S(1)} %broadcast_in_dim.34), channel_id=1, replica_groups=mesh['ba'=16,'ha'=8] {'ha'}, dimensions={0} | all-to-all | bytes 2359296 | tf_op jit(solution)/shard_map/all_to_all | solution.py:26
  437.7 0.5 fusion.18
  438.2 1.6 reshape.35
  439.7 6.3 %all-to-all-start.2 = ((f32[16,36,896]{2,1,0:T(8,128)}), f32[16,36,896]{2,1,0:T(8,128)}, u32[]{:S(2)}, u32[]{:S(2)}) async-start(f32[16,36,896]{2,1,0:T(8,128)} %reshape.35), calls=%async_computation.2 | async-start | bytes 4587520 | tf_op jit(solution)/shard_map/all_to_all | solution.py:20
  446.0 2.9 multiply_convert_fusion
  448.9 2.6 copy.22
  451.5 4.6 copy.24
  456.1 1.0 convolution_convert_fusion
  457.1 19.0 %all-to-all-done.2 = f32[16,36,896]{2,1,0:T(8,128)} async-done(((f32[16,36,896]{2,1,0:T(8,128)}), f32[16,36,896]{2,1,0:T(8,128)}, u32[]{:S(2)}, u32[]{:S(2)}) %all-to-all-start.2) | async-done | bytes 2064416 | tf_op jit(solution)/shard_map/all_to_all | solution.py:20
  476.1 2.4 reduce_sum.42
  (49 shorter events, 0.7 us)
Async XLA Ops:
  7.2 449.0 %copy-start = (bf16[576,896]{1,0:T(8,128)(2,1)S(1)}, bf16[576,896]{1,0:T(8,128)(2,1)}, u32[]{:S(2)}) copy-start(bf16[576,896]{1,0:T(8,128)(2,1)} %param.17) | copy-start | bytes 3096580
  7.2 307.9 %all-gather.2.cloned.1.call-start = ((), (), s32[]{:S(2)}) async-start(), calls=%async_computation.3 | async-start | bytes 1320960 | tf_op jit(solution)/shard_map/all_gather | solution.py:68
  8.8 8.1 %copy-start.4 = (f32[256,8]{1,0:T(8,128)}, f32[256,8]{1,0:T(8,128)S(1)}, u32[]{:S(2)}) copy-start(f32[256,8]{1,0:T(8,128)S(1)} %copy.21) | copy-start | bytes 24580
  11.8 303.3 %copy-start.1 = (bf16[256,8,512]{2,1,0:T(8,128)(2,1)S(1)}, bf16[256,8,512]{2,1,0:T(8,128)(2,1)}, u32[]{:S(2)}) copy-start(bf16[256,8,512]{2,1,0:T(8,128)(2,1)} %param.11) | copy-start | bytes 6291460
  11.8 303.3 %copy-start.6 = (s32[256]{0:T(256)S(1)}, s32[256]{0:T(256)}, u32[]{:S(2)}) copy-start(s32[256]{0:T(256)} %param.14) | copy-start | bytes 3076
  320.4 5.0 %slice-start = ((s8[4718592]{0:T(1024)(128)(4,1)}), s8[4194304]{0:T(1024)(128)(4,1)S(1)}, s32[]{:S(2)}) async-start(s8[4718592]{0:T(1024)(128)(4,1)} %bitcast.74), calls=%async_computation.4 | async-start | bytes 8388608 | tf_op jit(solution)/shard_map/while
  321.4 2.0 copy-start.3
  321.4 4.0 slice-start.1
  326.7 2.1 copy-start.2
  334.2 5.0 %slice-start = ((s8[4718592]{0:T(1024)(128)(4,1)}), s8[4194304]{0:T(1024)(128)(4,1)S(1)}, s32[]{:S(2)}) async-start(s8[4718592]{0:T(1024)(128)(4,1)} %bitcast.74), calls=%async_computation.4 | async-start | bytes 8388608 | tf_op jit(solution)/shard_map/while
  335.2 2.0 copy-start.3
  335.2 4.0 slice-start.1
  340.5 2.1 copy-start.2
  348.0 5.0 %slice-start = ((s8[4718592]{0:T(1024)(128)(4,1)}), s8[4194304]{0:T(1024)(128)(4,1)S(1)}, s32[]{:S(2)}) async-start(s8[4718592]{0:T(1024)(128)(4,1)} %bitcast.74), calls=%async_computation.4 | async-start | bytes 8388608 | tf_op jit(solution)/shard_map/while
  349.0 2.0 copy-start.3
  349.0 4.0 slice-start.1
  354.3 2.1 copy-start.2
  361.8 5.0 %slice-start = ((s8[4718592]{0:T(1024)(128)(4,1)}), s8[4194304]{0:T(1024)(128)(4,1)S(1)}, s32[]{:S(2)}) async-start(s8[4718592]{0:T(1024)(128)(4,1)} %bitcast.74), calls=%async_computation.4 | async-start | bytes 8388608 | tf_op jit(solution)/shard_map/while
  362.7 2.0 copy-start.3
  362.7 4.0 slice-start.1
  368.1 2.1 copy-start.2
  413.0 24.7 %copy-start.5 = (bf16[64,896]{1,0:T(8,128)(2,1)S(1)}, bf16[64,896]{1,0:T(8,128)(2,1)}, u32[]{:S(2)}) copy-start(bf16[64,896]{1,0:T(8,128)(2,1)} %param.16) | copy-start | bytes 344068
  439.7 36.4 %all-to-all-start.2 = ((f32[16,36,896]{2,1,0:T(8,128)}), f32[16,36,896]{2,1,0:T(8,128)}, u32[]{:S(2)}, u32[]{:S(2)}) async-start(f32[16,36,896]{2,1,0:T(8,128)} %reshape.35), calls=%async_computation.2 | async-start | bytes 4587520 | tf_op jit(solution)/shard_map/all_to_all | solution.py:20
Sparse Core Ops, SparseCore 0:
  9.7 305.3 all-gather.1
where the time goes:
time: 486 us; the launch traced here: 485 us
  waiting for transfers between devices  318 us (65%)
  blocking collectives  62.2 us (13%)
  local copies, waits for them, and re-layouts  38.8 us (8%)
  matrix products  32.9 us (7%)
  between operations  14.1 us (3%)
  other arithmetic  12.7 us (3%)
  starting transfers between devices  6.3 us (1%)
    all_gather x1, waiting for transfers between devices, on_device(): all_keys = lax.all_gather(latents, ('ba', 'ha'), axis=0, tiled=True)  298 us
    all_to_all x1, blocking collectives, sent_and_summed(): lax.all_to_all(cut_along(shard, dim, peers), axis, 0, 0, tiled=True)  37.6 us
    all_to_all x1, blocking collectives, from_everyone(): lax.all_to_all(jnp.broadcast_to(shard[None], (peers, *shard.shape)), axis...  24.6 us
    all_to_all x1, waiting for transfers between devices, sent_and_summed(): lax.all_to_all(cut_along(shard, dim, peers), axis, 0, 0, tiled=True)  19 us
    while x32, local copies, waits for them, and re-layouts  13.5 us
    dot_general x4, matrix products, tile_terms(): jnp.einsum('qd,kd->qk', query_rows, key_block, preferred_element_type=jnp...  11.4 us
    unnamed x13, local copies, waits for them, and re-layouts  10.5 us
  transfers between devices with their start and end apart: 2, of which 2 were waited for; matrix products, arithmetic and copies ran while one was open for 4% of the time, Pallas kernels for 0%

commit v1 on v0

v1 whole, which is shorter than its diff:
```python
import jax
import jax.numpy as jnp
from jax import lax
from jax.experimental import pallas as pl
from jax.experimental.pallas import tpu as pltpu
from jax.sharding import PartitionSpec as P

MESH = pl.DeviceIdType.MESH
SCALE = 192.0 ** (-0.5)
RANK = 512
KT = 256
NT = (((1,), (1,)), ((), ()))
NN = (((1,), (0,)), ((), ()))
F32 = jnp.float32
BF = jnp.bfloat16

def attn_kernel(par_ref, q_ref, do_ref, os_ref, lse_ref, k_ref, dq_ref, part_ref, kt_ref, acc_ref, dqt_ref, p_s, ds_s):
    b = pl.program_id(0)
    nb = pl.num_programs(0)
    keys = k_ref.shape[0]
    rows = q_ref.shape[0]

    @pl.when(b == 0)
    def _():
        acc_ref[...] = jnp.zeros_like(acc_ref)
        for i in range(keys // KT):
            kt_ref[:, i * KT:(i + 1) * KT] = k_ref[i * KT:(i + 1) * KT, :].T

    prod = do_ref[...].astype(F32) * os_ref[...].astype(F32)
    part = prod[:, 0:128]
    for i in range(1, RANK // 128):
        part = part + prod[:, i * 128:(i + 1) * 128]
    delta = jnp.sum(part.T, axis=0, keepdims=True) * SCALE
    lse = lse_ref[pl.ds(b, 1), :]
    limit = par_ref[b * (par_ref.shape[0] // nb)]
    count = limit // KT + 1
    dqt_ref[...] = jnp.zeros_like(dqt_ref)

    def tile(i, _):
        at = pl.multiple_of(i * KT, KT)
        kb = k_ref[pl.ds(at, KT), :]
        s = lax.dot_general(kb, q_ref[...], NT, preferred_element_type=F32)
        g = lax.dot_general(kb[:, :RANK], do_ref[...], NT, preferred_element_type=F32)
        idx = at + lax.broadcasted_iota(jnp.int32, (KT, 1), 0)
        p = jnp.where(idx <= limit, jnp.exp(s * SCALE - lse), 0.0)
        ds = (p * (g * SCALE - delta)).astype(BF)
        pb = p.astype(BF)
        acc_ref[pl.ds(at, KT), :] += lax.dot_general(ds, q_ref[...], NN, preferred_element_type=F32)
        acc_ref[pl.ds(at, KT), :RANK] += lax.dot_general(pb, do_ref[...], NN, preferred_element_type=F32)
        dqt_ref[...] += lax.dot_general(kt_ref[:, pl.ds(at, KT)], ds, NN, preferred_element_type=F32)
        return 0

    lax.fori_loop(0, count, tile, 0)
    dq_ref[...] = dqt_ref[...].T.astype(BF)

    @pl.when(b == nb - 1)
    def _():
        part_ref[...] = acc_ref[...].astype(BF)


def attn(parents, q, do, osv, lse, k):
    rows, width = q.shape
    keys = k.shape[0]
    nb = 8
    rb = rows // nb
    return pl.pallas_call(
        attn_kernel,
        grid_spec=pltpu.PrefetchScalarGridSpec(
            num_scalar_prefetch=1,
            grid=(nb,),
            in_specs=[
                pl.BlockSpec((rb, width), lambda b, p: (b, 0)),
                pl.BlockSpec((rb, RANK), lambda b, p: (b, 0)),
                pl.BlockSpec((rb, RANK), lambda b, p: (b, 0)),
                pl.BlockSpec((nb, rb), lambda b, p: (0, 0)),
                pl.BlockSpec((keys, width), lambda b, p: (0, 0)),
            ],
            out_specs=[
                pl.BlockSpec((rb, width), lambda b, p: (b, 0)),
                pl.BlockSpec((keys, width), lambda b, p: (0, 0)),
            ],
            scratch_shapes=[
                pltpu.VMEM((width, keys), BF),
                pltpu.VMEM((keys, width), F32),
                pltpu.VMEM((width, rb), F32),
                pltpu.VMEM((KT, rb), BF),
                pltpu.VMEM((KT, rb), BF),
            ],
        ),
        out_shape=[
            jax.ShapeDtypeStruct((rows, width), BF),
            jax.ShapeDtypeStruct((keys, width), BF),
        ],
        compiler_params=pltpu.CompilerParams(dimension_semantics=("arbitrary",)),
    )(parents, q, do, osv, lse, k)


def place():
    ba, ha = lax.axis_index("ba"), lax.axis_index("ha")
    core = lax.rem(ba, 2)
    z = lax.rem(ba // 2, 4)
    ylo = ba // 8
    x = lax.rem(ha, 4)
    yhi = ha // 4
    return core, x, yhi, ylo, z


def device(core, x, y, z):
    return {"ba": (lax.rem(y, 2) * 4 + z) * 2 + core, "ha": (y // 2) * 4 + x}


def meet(peers):
    barrier = pltpu.get_barrier_semaphore()
    for peer in peers:
        pl.semaphore_signal(barrier, inc=1, device_id=peer, device_id_type=MESH)
    pl.semaphore_wait(barrier, len(peers))


def send(src, dst, send_sem, recv_sem, peer):
    return pltpu.make_async_remote_copy(
        src_ref=src, dst_ref=dst, send_sem=send_sem, recv_sem=recv_sem,
        device_id=peer, device_id_type=MESH,
    )


def gather_kernel(lat_ref, out_ref, plane_s, plane_r, line_s, line_r, pair_s, pair_r):
    core, x, yhi, ylo, z = place()
    y = yhi * 2 + ylo
    first = core == 0
    u, w = jnp.where(first, x, z), jnp.where(first, z, x)

    def at(du, dy, dw):
        pu, pw = lax.rem(u + du, 4), lax.rem(w + dw, 4)
        return device(core, jnp.where(first, pu, pw), lax.rem(y + dy, 4), jnp.where(first, pw, pu))

    partner = device(1 - core, x, y, z)
    plane = [(du, dy) for dy in range(4) for du in range(4) if du or dy]
    plane.sort(key=lambda d: -(min(d[0], 4 - d[0]) + min(d[1], 4 - d[1])))
    meet([at(du, dy, 0) for du, dy in plane] + [at(0, 0, dw) for dw in (1, 2, 3)] + [partner])
    mine = out_ref.at[ylo, z, core, yhi, x]
    copies = []
    for n, (du, dy) in enumerate(plane):
        copy = send(lat_ref, mine, plane_s.at[n], plane_r.at[n], at(du, dy, 0))
        copy.start()
        copies.append(copy)
    out_ref[ylo, z, core, yhi, x] = lat_ref[...]
    for copy in copies:
        copy.wait_recv()

    for c in (0, 1):
        def block(k):
            return out_ref.at[:, k, 0] if c == 0 else out_ref.at[:, :, 1, :, k]

        @pl.when(core == c)
        def _():
            line, pair = [], []
            for n, dw in enumerate((2, 1, 3)):
                copy = send(block(w), block(w), line_s.at[n], line_r.at[n], at(0, 0, dw))
                copy.start()
                line.append(copy)
            own = send(block(w), block(w), pair_s.at[3], pair_r.at[3], partner)
            own.start()
            pair.append(own)
            for n, dw in ((1, 1), (2, 3), (0, 2)):
                line[n].wait_recv()
                src = lax.rem(w + 4 - dw, 4)
                copy = send(block(src), block(src), pair_s.at[n], pair_r.at[n], partner)
                copy.start()
                pair.append(copy)
            for copy in line + pair:
                copy.wait_send()
            for copy in pair:
                copy.wait_recv()

    for copy in copies:
        copy.wait_send()


def gather(latents):
    rows, width = latents.shape
    return pl.pallas_call(
        gather_kernel,
        out_shape=jax.ShapeDtypeStruct((2, 4, 2, 2, 4, rows, width), latents.dtype),
        in_specs=[pl.BlockSpec(memory_space=pltpu.VMEM)],
        out_specs=pl.BlockSpec(memory_space=pltpu.VMEM),
        scratch_shapes=[pltpu.SemaphoreType.DMA((n,)) for n in (15, 15, 3, 3, 4, 4)],
        compiler_params=pltpu.CompilerParams(collective_id=0, has_side_effects=True),
    )(latents)


def total(*blocks):
    out = blocks[0].astype(F32)
    for block in blocks[1:]:
        out = out + block.astype(F32)
    return out


def reduce_kernel(part_ref, hid_ref, rows_ref, cols_ref, hall_ref,
                  got0, acc0, got1, acc1, got2, acc2, colbuf, gotr, gotc,
                  s0, r0, s1, r1, s2, r2, s3, r3, s3c, r3c, s4, r4, s4c, r4c, sh, rh, sp, rp, lsem):
    core, x, yhi, ylo, z = place()
    y = yhi * 2 + ylo
    g, ha = ylo * 4 + z, yhi * 4 + x
    partner = device(1 - core, x, y, z)
    heads = [(dy, dx) for dy in (0, 1) for dx in range(4) if dy or dx]
    heads.sort(key=lambda d: -(2 * d[0] + min(d[1], 4 - d[1])))
    chips = [(dy, dz) for dy in (0, 1) for dz in range(4) if dy or dz]
    chips.sort(key=lambda d: -(d[0] + min(d[1], 4 - d[1])))

    def head_at(dy, dx):
        py, px = lax.rem(yhi + dy, 2), lax.rem(x + dx, 4)
        return py * 4 + px, device(core, px, py * 2 + ylo, z)

    def chip_at(dy, dz):
        py, pz = lax.rem(ylo + dy, 2), lax.rem(z + dz, 4)
        return py * 4 + pz, device(core, x, yhi * 2 + py, pz)

    meet([partner] + [head_at(*d)[1] for d in heads] + [chip_at(*d)[1] for d in chips])

    pending = []
    for c in (0, 1):
        @pl.when(core == c)
        def _():
            send(part_ref.at[:, 1 - c], got0, s0, r0, partner).start()
    first = send(part_ref.at[:, 0], got0, s0, r0, partner)
    own_hidden = pltpu.make_async_copy(hid_ref, hall_ref.at[core, :, g], lsem)
    own_hidden.start()
    hidden = []
    for n, d in enumerate(chips):
        copy = send(hid_ref, hall_ref.at[core, :, g], sh.at[n], rh.at[n], chip_at(*d)[1])
        copy.start()
        hidden.append(copy)
    first.wait_recv()

    for px in range(4):
        for py in range(2):
            acc0[px, py] = total(part_ref[:, core, py, px], got0[:, py, px]).astype(BF)

    line = []
    for n, dx in enumerate((2, 1, 3)):
        to, peer = head_at(0, dx)
        copy = send(acc0.at[to - yhi * 4], got1.at[n], s1.at[n], r1.at[n], peer)
        copy.start()
        line.append(copy)
    for copy in line:
        copy.wait_recv()
    for py in range(2):
        acc1[py] = total(acc0[x, py], got1[0, py], got1[1, py], got1[2, py]).astype(BF)
    other = send(acc1.at[1 - yhi], got2, s2, r2, head_at(1, 0)[1])
    other.start()
    other.wait_recv()
    summed = total(acc1[yhi], got2[...])
    acc2[...] = summed.astype(BF)
    colbuf[...] = jnp.zeros_like(colbuf)
    flat = summed.reshape(64, summed.shape[-1])
    for k in range(8):
        colbuf[k, :, 0:72] = flat[:, k * 72:(k + 1) * 72].astype(BF)
    rows, cols = [], []
    for n, d in enumerate(chips):
        to, peer = chip_at(*d)
        copy = send(acc2.at[to], gotr.at[n], s3.at[n], r3.at[n], peer)
        copy.start()
        rows.append(copy)
        copy = send(colbuf.at[to], gotc.at[n], s3c.at[n], r3c.at[n], peer)
        copy.start()
        cols.append(copy)
    for copy in hidden:
        copy.wait_recv()
    own_hidden.wait()
    swap = send(hall_ref.at[core], hall_ref.at[core], sp.at[0], rp.at[0], partner)
    swap.start()
    for copy in rows + cols:
        copy.wait_recv()
    rows_ref[ha] = total(acc2[g], *[gotr[n] for n in range(7)]).astype(BF)
    cols_ref[core, ha] = total(colbuf[g], *[gotc[n] for n in range(7)]).astype(BF)
    spread = []
    for n, d in enumerate(heads):
        _, peer = head_at(*d)
        copy = send(rows_ref.at[ha], rows_ref.at[ha], s4.at[n], r4.at[n], peer)
        copy.start()
        spread.append(copy)
        copy = send(cols_ref.at[core, ha], cols_ref.at[core, ha], s4c.at[n], r4c.at[n], peer)
        copy.start()
        spread.append(copy)
    for copy in spread:
        copy.wait_recv()
    last = send(cols_ref.at[core], cols_ref.at[core], sp.at[1], rp.at[1], partner)
    last.start()
    first.wait_send()
    for copy in hidden + line + [other] + rows + cols + spread:
        copy.wait_send()
    swap.wait()
    last.wait()


def reduce_and_spread(part, hidden):
    width, columns = part.shape[-1], hidden.shape[-1]
    dma = pltpu.SemaphoreType.DMA
    return pl.pallas_call(
        reduce_kernel,
        out_shape=[
            jax.ShapeDtypeStruct((8, 8, width), BF),
            jax.ShapeDtypeStruct((2, 8, 64, 128), BF),
            jax.ShapeDtypeStruct((2, 8, 8, 8, columns), BF),
        ],
        in_specs=[pl.BlockSpec(memory_space=pltpu.VMEM)] * 2,
        out_specs=[pl.BlockSpec(memory_space=pltpu.VMEM)] * 3,
        scratch_shapes=[
            pltpu.VMEM((8, 2, 4, 8, width), BF),
            pltpu.VMEM((4, 2, 8, 8, width), BF),
            pltpu.VMEM((3, 2, 8, 8, width), BF),
            pltpu.VMEM((2, 8, 8, width), BF),
            pltpu.VMEM((8, 8, width), BF),
            pltpu.VMEM((8, 8, width), BF),
            pltpu.VMEM((8, 64, 128), BF),
            pltpu.VMEM((7, 8, width), BF),
            pltpu.VMEM((7, 64, 128), BF),
            dma, dma, dma((3,)), dma((3,)), dma, dma, dma((7,)), dma((7,)), dma((7,)), dma((7,)),
            dma((7,)), dma((7,)), dma((7,)), dma((7,)), dma((7,)), dma((7,)), dma((2,)), dma((2,)), dma,
        ],
        compiler_params=pltpu.CompilerParams(collective_id=1, has_side_effects=True),
    )(part, hidden)


def on_device(queries, out_grad, out_saved, logsumexp, parents, latents, hidden, latent_weight):
    tokens, heads, width = queries.shape
    rows = tokens * heads
    keys = gather(latents).reshape(-1, width)
    query_grad, part = attn(
        parents, queries.reshape(rows, width), out_grad.reshape(rows, RANK),
        out_saved.reshape(rows, RANK), logsumexp.reshape(8, rows // 8), keys,
    )
    row_block, cols, hidden_all = reduce_and_spread(
        part.reshape(8, 2, 2, 4, 8, width), hidden.reshape(8, 8, -1)
    )
    core = lax.rem(lax.axis_index("ba"), 2)
    cols = lax.dynamic_slice_in_dim(cols.reshape(1024, 128), core * 36, 36, axis=1)
    weight_grad = lax.dot_general(
        cols, hidden_all.reshape(1024, -1), (((0,), (0,)), ((), ())), preferred_element_type=F32
    ).astype(BF)
    input_grad = jnp.dot(
        row_block.reshape(64, width), latent_weight, preferred_element_type=F32
    ).astype(BF)
    return query_grad.reshape(tokens, heads, width), weight_grad, input_grad


def solution(mesh):
    return jax.shard_map(
        on_device,
        mesh=mesh,
        in_specs=(
            P("ba", "ha", None),
            P("ba", "ha", None),
            P("ba", "ha", None),
            P("ba", "ha"),
            P("ba"),
            P(("ba", "ha"), None),
            P("ba", "ha"),
            P(None, "ha"),
        ),
        out_specs=(P("ba", "ha", None), P("ba", "ha"), P("ba", "ha")),
        check_vma=False,
    )
```

time: 486 us -> 97.6 us (0.20)
  waiting for transfers between devices: 318 us -> 0 us
  Pallas kernels: 0 us -> 80.8 us
  blocking collectives: 62.2 us -> 0 us
  matrix products: 32.9 us -> 3.79 us
  local copies, waits for them, and re-layouts: 38.8 us -> 10.5 us
  between operations: 14.1 us -> 0.69 us
  other arithmetic: 12.7 us -> 0 us
  starting transfers between devices: 6.3 us -> 0 us
    all_gather x1 -> x0, waiting for transfers between devices: 298 us -> none  [on_device(): all_keys = lax.all_gather(latents, ('ba', 'ha'), axis=0, tiled=True)]
    pallas_call x0 -> x3, Pallas kernels: none -> 80.8 us  [the longest x1 41.4 us: reduce_and_spread(): pl.pallas_call(reduce_kernel, out_shape=[jax.ShapeDtypeStruct((8, 8, widt...]
    all_to_all x2 -> x0, blocking collectives: 62.2 us -> none  [the longest x1 37.6 us: sent_and_summed(): lax.all_to_all(cut_along(shard, dim, peers), axis, 0, 0, tiled=True)]
    dot_general x22 -> x2, matrix products: 32.9 us -> 3.79 us  [the longest x1 2.83 us: on_device(): lax.dot_general(cols, hidden_all.reshape(1024, -1), (((0,), (0,)), ((), (...]
    all_to_all x1 -> x0, waiting for transfers between devices: 19 us -> none  [sent_and_summed(): lax.all_to_all(cut_along(shard, dim, peers), axis, 0, 0, tiled=True)]
    while x33 -> x0, local copies, waits for them, and re-layouts: 16.7 us -> none
    reduce_sum x4 -> x0, other arithmetic: 7.21 us -> none  [the longest x2 4.29 us: sent_and_summed(): return jnp.sum(pieces, axis=0)]
    all_to_all x1 -> x0, starting transfers between devices: 6.26 us -> none  [sent_and_summed(): lax.all_to_all(cut_along(shard, dim, peers), axis, 0, 0, tiled=True)]
  transfers between devices with their start and end apart: 2 -> 0, of which waited for: 2 -> 0; matrix products, arithmetic and copies ran while one was open for 4% -> 0% of each run, Pallas kernels for 0% -> 0%
where the time goes in v1:
time: 97.6 us; the launch traced here: 95.8 us
  Pallas kernels  80.8 us (83%)
  local copies, waits for them, and re-layouts  10.5 us (11%)
  matrix products  3.79 us (4%)
    pallas_call x1, Pallas kernels, reduce_and_spread(): pl.pallas_call(reduce_kernel, out_shape=[jax.ShapeDtypeStruct((8, 8, widt...  41.4 us
    pallas_call x1, Pallas kernels, gather(): pl.pallas_call(gather_kernel, out_shape=jax.ShapeDtypeStruct((2, 4, 2, 2,...  23.4 us
    pallas_call x1, Pallas kernels, attn(): pl.pallas_call(attn_kernel, grid_spec=pltpu.PrefetchScalarGridSpec(num_sc...  16 us
    unnamed x9, local copies, waits for them, and re-layouts  9.76 us
    dot_general x1, matrix products, on_device(): lax.dot_general(cols, hidden_all.reshape(1024, -1), (((0,), (0,)), ((), (...  2.83 us

profile of v1, /device:TPU:1, one launch (start us, length us, event | category | flops | bytes accessed | tf_op | source)
XLA Modules:
  0.0 95.8 jit_solution(2779987048234008934)
XLA Ops:
  0.6 0.0 copy-start
  0.6 0.0 copy-start.2
  0.7 5.0 %copy.14 = bf16[256,8,576]{2,1,0:T(8,128)(2,1)} copy(bf16[256,8,576]{0,2,1:T(8,128)(2,1)} %param.8) | data formatting | bytes 4718592 | tf_op args[0]
  5.6 0.0 copy-done.2
  5.6 0.1 copy.15
  5.8 0.7 reshape.42.lse_ref
  6.5 23.4 %shard_map.103 = bf16[2,4,2,2,4,8,576]{6,5,4,3,2,1,0:T(8,128)(2,1)} custom-call(bf16[8,576]{1,0:T(8,128)(2,1)} %lat_ref.1), custom_call_target="tpu_custom_call" | custom-call | tf_op jit(solution)/shard_map/pallas_call | solution.py:181
  29.9 16.0 %shard_map.104 = (bf16[2048,576]{1,0:T(8,128)(2,1)}, bf16[1024,576]{1,0:T(8,128)(2,1)}) custom-call(s32[256]{0:T(256)} %par_ref.1, bf16[2048,576]{1,0:T(8,128)(2,1)} %bitcast.14, bf16[2048,512]{1,0:T(8,128)(2,1)} %bitcast.17, bf16[2048,512]{1,0:T(8,128)(2,1)} %bitcast.18, f32[8,256]{1,0:T(8,128)} %reshape.42.lse_ref, bf16[1024,576]{1,0:T(8,128)(2,1)} %bitcast.15), custom_call_target="tpu_custom_call" | custom-call | tf_op jit(solution)/shard_map/pallas_call | solution.py:66
  45.9 4.6 %copy.16 = bf16[256,8,576]{0,2,1:T(8,128)(2,1)} copy(bf16[256,8,576]{2,1,0:T(8,128)(2,1)} %bitcast.16) | data formatting | bytes 4718592
  50.5 41.4 %shard_map.105 = (bf16[8,8,576]{2,1,0:T(8,128)(2,1)}, bf16[2,8,64,128]{3,2,1,0:T(8,128)(2,1)}, bf16[2,8,8,8,896]{4,3,2,1,0:T(8,128)(2,1)}) custom-call(bf16[8,2,2,4,8,576]{5,4,3,2,1,0:T(8,128)(2,1)} %bitcast.20, bf16[8,8,896]{2,1,0:T(8,128)(2,1)} %bitcast.22), custom_call_target="tpu_custom_call" | custom-call | tf_op jit(solution)/shard_map/pallas_call | solution.py:299
  92.0 0.0 copy-start.1
  92.0 2.8 %convolution_convert_fusion.1 = bf16[36,896]{1,0:T(8,128)(2,1)} fusion(bf16[1024,896]{1,0:T(8,128)(2,1)} %bitcast.19, bf16[1024,128]{1,0:T(8,128)(2,1)} %bitcast.21, s32[]{:T(128)S(6)} %select_n.3), kind=kOutput, calls=%fused_computation.1 | convolution fusion | flops 66092544 | bytes 2161668 | tf_op jit(solution)/shard_map/dot_general | solution.py:338
  94.8 0.0 copy-done
  94.8 0.0 copy-done.1
  94.8 1.0 convolution_convert_fusion
Async XLA Ops:
  0.6 94.2 %copy-start = (bf16[576,896]{1,0:T(8,128)(2,1)S(1)}, bf16[576,896]{1,0:T(8,128)(2,1)}, u32[]{:S(2)}) copy-start(bf16[576,896]{1,0:T(8,128)(2,1)} %param.15) | copy-start | bytes 3096580
  0.6 5.0 %copy-start.2 = (f32[256,8]{0,1:T(8,128)S(1)}, f32[256,8]{0,1:T(8,128)}, u32[]{:S(2)}) copy-start(f32[256,8]{0,1:T(8,128)} %param.11) | copy-start | bytes 24580
  92.0 2.9 %copy-start.1 = (bf16[8,8,576]{2,1,0:T(8,128)(2,1)S(1)}, bf16[8,8,576]{2,1,0:T(8,128)(2,1)}, u32[]{:S(2)}) copy-start(bf16[8,8,576]{2,1,0:T(8,128)(2,1)} %get-tuple-element.12) | copy-start | bytes 221188

commit v2 on v1

v2 whole, which is shorter than its diff:
```python
import jax
import jax.numpy as jnp
from jax import lax
from jax.experimental import pallas as pl
from jax.experimental.pallas import tpu as pltpu
from jax.sharding import PartitionSpec as P

MESH = pl.DeviceIdType.MESH
SCALE = 192.0 ** (-0.5)
RANK = 512
KT = 256
NT = (((1,), (1,)), ((), ()))
NN = (((1,), (0,)), ((), ()))
F32 = jnp.float32
BF = jnp.bfloat16

def attn_kernel(par_ref, qt_ref, do_ref, ld_ref, k_ref, dq_ref, part_ref, acc_ref, kt_ref, dqt_ref, p0, d0, p1, d1):
    nb = qt_ref.shape[0]
    keys = k_ref.shape[0]
    per = par_ref.shape[0] // nb
    acc_ref[...] = jnp.zeros_like(acc_ref)
    p1[...] = jnp.zeros_like(p1)
    d1[...] = jnp.zeros_like(d1)
    for i in range(keys // KT):
        kt_ref[:, i * KT:(i + 1) * KT] = k_ref[i * KT:(i + 1) * KT, :].T

    def limit_of(b):
        return jnp.where(b < nb, par_ref[jnp.minimum(b, nb - 1) * per], -1)

    def step(b, t, ob, ot, fresh, p_in, d_in, p_out, d_out):
        limit = limit_of(b)
        bb = jnp.minimum(b, nb - 1)
        at = pl.multiple_of(t * KT, KT)
        s = lax.dot_general(k_ref[pl.ds(at, KT), :], qt_ref[bb], NN, preferred_element_type=F32)
        g = lax.dot_general(k_ref[pl.ds(at, KT), :RANK], do_ref[bb], NT, preferred_element_type=F32)
        idx = at + lax.broadcasted_iota(jnp.int32, (KT, 1), 0)
        p = jnp.where(idx <= limit, jnp.exp(s * SCALE - ld_ref[0, pl.ds(bb, 1), :]), 0.0)
        d_out[...] = (p * (g * SCALE - ld_ref[1, pl.ds(bb, 1), :])).astype(BF)
        p_out[...] = p.astype(BF)

        oat = pl.multiple_of(ot * KT, KT)
        ds, pp = d_in[...], p_in[...]
        key = lax.dot_general(ds, qt_ref[ob], NT, preferred_element_type=F32)
        val = lax.dot_general(pp, do_ref[ob], NN, preferred_element_type=F32)
        acc_ref[pl.ds(oat, KT), :RANK] += key[:, :RANK] + val
        acc_ref[pl.ds(oat, KT), RANK:] += key[:, RANK:]
        dq = lax.dot_general(kt_ref[:, pl.ds(oat, KT)], ds, NN, preferred_element_type=F32)
        dqt_ref[ob] = dq + jnp.where(fresh, 0.0, dqt_ref[ob])
        more = (t + 1) * KT <= limit
        nextb = jnp.where(more, b, jnp.minimum(b + 1, nb))
        nextt = jnp.where(more, t + 1, 0)
        return nextb, nextt, bb, t, jnp.logical_and(t == 0, b < nb)

    def trip(_, carry):
        carry = step(*carry, p1, d1, p0, d0)
        return step(*carry, p0, d0, p1, d1)

    steps = 1
    for b in range(nb):
        steps = steps + par_ref[b * per] // KT + 1
    lax.fori_loop(0, (steps + 1) // 2, trip, (0, 0, 0, 0, False))

    for b in range(nb):
        block = dqt_ref[b].astype(BF)
        width = block.shape[1] // nb
        for h in range(nb):
            dq_ref[h, :, b * width:(b + 1) * width] = block[:, h * width:(h + 1) * width]
    part_ref[...] = acc_ref[...].astype(BF)


def core_attn(parents, qt, do, ld, k):
    nb, width, rb = qt.shape
    keys = k.shape[0]
    vm = pl.BlockSpec(memory_space=pltpu.VMEM)
    return pl.pallas_call(
        attn_kernel,
        in_specs=[pl.BlockSpec(memory_space=pltpu.SMEM)] + [vm] * 4,
        out_specs=[vm] * 3,
        scratch_shapes=[
            pltpu.VMEM((width, keys), BF),
            pltpu.VMEM((nb, width, rb), F32),
        ] + [pltpu.VMEM((KT, rb), BF)] * 4,
        out_shape=[
            jax.ShapeDtypeStruct((nb, width, rb), BF),
            jax.ShapeDtypeStruct((keys, width), BF),
            jax.ShapeDtypeStruct((keys, width), F32),
        ],
        compiler_params=pltpu.CompilerParams(vmem_limit_bytes=32 * 2**20),
    )(parents, qt, do, ld, k)

def place():
    ba, ha = lax.axis_index("ba"), lax.axis_index("ha")
    core = lax.rem(ba, 2)
    z = lax.rem(ba // 2, 4)
    ylo = ba // 8
    x = lax.rem(ha, 4)
    yhi = ha // 4
    return core, x, yhi, ylo, z


def device(core, x, y, z):
    return {"ba": (lax.rem(y, 2) * 4 + z) * 2 + core, "ha": (y // 2) * 4 + x}


def meet(peers):
    barrier = pltpu.get_barrier_semaphore()
    for peer in peers:
        pl.semaphore_signal(barrier, inc=1, device_id=peer, device_id_type=MESH)
    pl.semaphore_wait(barrier, len(peers))


def send(src, dst, send_sem, recv_sem, peer):
    return pltpu.make_async_remote_copy(
        src_ref=src, dst_ref=dst, send_sem=send_sem, recv_sem=recv_sem,
        device_id=peer, device_id_type=MESH,
    )


def prepare(b, perm, q_in, do_in, os_in, lse_ref, qt_ref, do_ref, ld_ref):
    heads, tokens = lse_ref.shape
    run = tokens // heads
    lanes = slice(b * run, (b + 1) * run)
    qt_ref[b] = jnp.concatenate([q_in[h, :, lanes] for h in range(heads)], axis=1)
    rows = slice(b * tokens, (b + 1) * tokens)
    grad = lax.dot_general(perm, do_in[rows, :], NN, preferred_element_type=F32)
    saved = lax.dot_general(perm, os_in[rows, :], NN, preferred_element_type=F32)
    do_ref[b] = grad.astype(BF)
    prod = grad * saved
    part = prod[:, 0:128]
    for i in range(1, RANK // 128):
        part = part + prod[:, i * 128:(i + 1) * 128]
    ld_ref[0, b:b + 1, :] = jnp.concatenate([lse_ref[h:h + 1, lanes] for h in range(heads)], axis=1)
    ld_ref[1, b:b + 1, :] = jnp.sum(part.T, axis=0, keepdims=True) * SCALE


def gather_kernel(lat_ref, lse_ref, q_hbm, do_hbm, os_hbm, out_ref, qt_ref, do_ref, ld_ref,
                  q_in, do_in, os_in, plane_s, plane_r, line_s, line_r, pair_s, pair_r, load_s):
    loads = [
        pltpu.make_async_copy(src, dst, load_s.at[n])
        for n, (src, dst) in enumerate(((q_hbm, q_in), (do_hbm, do_in), (os_hbm, os_in)))
    ]
    for load in loads:
        load.start()
    core, x, yhi, ylo, z = place()
    y = yhi * 2 + ylo
    first = core == 0
    u, w = jnp.where(first, x, z), jnp.where(first, z, x)

    def at(du, dy, dw):
        pu, pw = lax.rem(u + du, 4), lax.rem(w + dw, 4)
        return device(core, jnp.where(first, pu, pw), lax.rem(y + dy, 4), jnp.where(first, pw, pu))

    partner = device(1 - core, x, y, z)
    plane = [(du, dy) for dy in range(4) for du in range(4) if du or dy]
    plane.sort(key=lambda d: -(min(d[0], 4 - d[0]) + min(d[1], 4 - d[1])))
    meet([at(du, dy, 0) for du, dy in plane] + [at(0, 0, dw) for dw in (1, 2, 3)] + [partner])
    mine = out_ref.at[ylo, z, core, yhi, x]
    copies = []
    for n, (du, dy) in enumerate(plane):
        copy = send(lat_ref, mine, plane_s.at[n], plane_r.at[n], at(du, dy, 0))
        copy.start()
        copies.append(copy)
    out_ref[ylo, z, core, yhi, x] = lat_ref[...]
    for load in loads:
        load.wait()
    heads, tokens = lse_ref.shape
    row = lax.broadcasted_iota(jnp.int32, (tokens, tokens), 0)
    col = lax.broadcasted_iota(jnp.int32, (tokens, tokens), 1)
    run = tokens // heads
    perm = jnp.where(col == lax.rem(row, run) * heads + row // run, 1.0, 0.0).astype(BF)
    for b in range(heads // 2):
        prepare(b, perm, q_in, do_in, os_in, lse_ref, qt_ref, do_ref, ld_ref)
    for copy in copies:
        copy.wait_recv()

    def block(c, k):
        return out_ref.at[:, k, 0] if c == 0 else out_ref.at[:, :, 1, :, k]

    def line_copy(c, n, dw):
        return send(block(c, w), block(c, w), line_s.at[n], line_r.at[n], at(0, 0, dw))

    def pair_copy(c, n, k):
        return send(block(c, k), block(c, k), pair_s.at[n], pair_r.at[n], partner)

    lines = ((2, 1, 3))
    for c in (0, 1):
        @pl.when(core == c)
        def _():
            for n, dw in enumerate(lines):
                line_copy(c, n, dw).start()
            pair_copy(c, 3, w).start()

    for b in range(heads // 2, heads):
        prepare(b, perm, q_in, do_in, os_in, lse_ref, qt_ref, do_ref, ld_ref)

    for c in (0, 1):
        @pl.when(core == c)
        def _():
            for n, dw in ((1, 1), (2, 3), (0, 2)):
                line_copy(c, n, dw).wait_recv()
                pair_copy(c, n, lax.rem(w + 4 - dw, 4)).start()
            for n, dw in enumerate(lines):
                line_copy(c, n, dw).wait_send()
            for n in range(4):
                pair_copy(c, n, w).wait()

    for copy in copies:
        copy.wait_send()


def gather(latents, lse, q, do, osv):
    rows, width = latents.shape
    heads, _, tokens = q.shape
    vm, hbm = pl.BlockSpec(memory_space=pltpu.VMEM), pl.BlockSpec(memory_space=pltpu.HBM)
    return pl.pallas_call(
        gather_kernel,
        out_shape=[
            jax.ShapeDtypeStruct((2, 4, 2, 2, 4, rows, width), BF),
            jax.ShapeDtypeStruct((heads, width, tokens), BF),
            jax.ShapeDtypeStruct((heads, tokens, RANK), BF),
            jax.ShapeDtypeStruct((2, heads, tokens), F32),
        ],
        in_specs=[vm, vm, hbm, hbm, hbm],
        out_specs=[vm] * 4,
        scratch_shapes=[pltpu.VMEM(a.shape, BF) for a in (q, do, osv)]
        + [pltpu.SemaphoreType.DMA((n,)) for n in (15, 15, 3, 3, 4, 4, 3)],
        compiler_params=pltpu.CompilerParams(
            collective_id=0, has_side_effects=True, vmem_limit_bytes=50 * 2**20
        ),
    )(latents, lse, q, do, osv)


def total(*blocks):
    out = blocks[0].astype(F32)
    for block in blocks[1:]:
        out = out + block.astype(F32)
    return out


def reduce_kernel(part_ref, own_ref, hid_ref, rows_ref, cols_ref, hall_ref,
                  got0, acc0, got1, acc1, keep1, got2, acc2, colbuf, gotr, gotc,
                  s0, r0, s1, r1, s2, r2, s3, r3, s3c, r3c, s4, r4, s4c, r4c, sh, rh, sp, rp, lsem):
    core, x, yhi, ylo, z = place()
    y = yhi * 2 + ylo
    g, ha = ylo * 4 + z, yhi * 4 + x
    partner = device(1 - core, x, y, z)
    heads = [(dy, dx) for dy in (0, 1) for dx in range(4) if dy or dx]
    heads.sort(key=lambda d: -(2 * d[0] + min(d[1], 4 - d[1])))
    chips = [(dy, dz) for dy in (0, 1) for dz in range(4) if dy or dz]
    chips.sort(key=lambda d: -(d[0] + min(d[1], 4 - d[1])))

    def head_at(dy, dx):
        py, px = lax.rem(yhi + dy, 2), lax.rem(x + dx, 4)
        return py * 4 + px, device(core, px, py * 2 + ylo, z)

    def chip_at(dy, dz):
        py, pz = lax.rem(ylo + dy, 2), lax.rem(z + dz, 4)
        return py * 4 + pz, device(core, x, yhi * 2 + py, pz)

    meet([partner] + [head_at(*d)[1] for d in heads] + [chip_at(*d)[1] for d in chips])

    pending = []
    for c in (0, 1):
        @pl.when(core == c)
        def _():
            send(part_ref.at[:, 1 - c], got0, s0, r0, partner).start()
    first = send(part_ref.at[:, 0], got0, s0, r0, partner)
    own_hidden = pltpu.make_async_copy(hid_ref, hall_ref.at[core, :, g], lsem)
    own_hidden.start()
    hidden = []
    for n, d in enumerate(chips):
        copy = send(hid_ref, hall_ref.at[core, :, g], sh.at[n], rh.at[n], chip_at(*d)[1])
        copy.start()
        hidden.append(copy)
    first.wait_recv()

    for px in range(4):
        for py in range(2):
            acc0[px, py] = total(own_ref[:, core, py, px], got0[:, py, px]).astype(BF)

    line = []
    for n, dx in enumerate((2, 1, 3)):
        to, peer = head_at(0, dx)
        copy = send(acc0.at[to - yhi * 4], got1.at[n], s1.at[n], r1.at[n], peer)
        copy.start()
        line.append(copy)
    for copy in line:
        copy.wait_recv()
    for py in range(2):
        summed = total(own_ref[:, core, py, x], got0[:, py, x], got1[0, py], got1[1, py], got1[2, py])
        keep1[py] = summed
        acc1[py] = summed.astype(BF)
    other = send(acc1.at[1 - yhi], got2, s2, r2, head_at(1, 0)[1])
    other.start()
    other.wait_recv()
    summed = total(keep1[yhi], got2[...])
    keep1[0] = summed
    acc2[...] = summed.astype(BF)
    flat = summed.reshape(64, summed.shape[-1])
    colbuf[...] = jnp.zeros_like(colbuf)
    for k in range(8):
        colbuf[k, :, 0:72] = flat[:, k * 72:(k + 1) * 72].astype(BF)
    rows, cols = [], []
    for n, d in enumerate(chips):
        to, peer = chip_at(*d)
        copy = send(acc2.at[to], gotr.at[n], s3.at[n], r3.at[n], peer)
        copy.start()
        rows.append(copy)
        copy = send(colbuf.at[to], gotc.at[n], s3c.at[n], r3c.at[n], peer)
        copy.start()
        cols.append(copy)
    for copy in hidden:
        copy.wait_recv()
    own_hidden.wait()
    swap = send(hall_ref.at[core], hall_ref.at[core], sp.at[0], rp.at[0], partner)
    swap.start()
    for copy in rows + cols:
        copy.wait_recv()
    rows_ref[ha] = total(keep1[0, g], *[gotr[n] for n in range(7)]).astype(BF)
    cols_ref[core, ha] = total(colbuf[g], *[gotc[n] for n in range(7)]).astype(BF)
    spread = []
    for n, d in enumerate(heads):
        _, peer = head_at(*d)
        copy = send(rows_ref.at[ha], rows_ref.at[ha], s4.at[n], r4.at[n], peer)
        copy.start()
        spread.append(copy)
        copy = send(cols_ref.at[core, ha], cols_ref.at[core, ha], s4c.at[n], r4c.at[n], peer)
        copy.start()
        spread.append(copy)
    for copy in spread:
        copy.wait_recv()
    last = send(cols_ref.at[core], cols_ref.at[core], sp.at[1], rp.at[1], partner)
    last.start()
    first.wait_send()
    for copy in hidden + line + [other] + rows + cols + spread:
        copy.wait_send()
    swap.wait()
    last.wait()


def reduce_and_spread(part, own, hidden):
    width, columns = part.shape[-1], hidden.shape[-1]
    dma = pltpu.SemaphoreType.DMA
    return pl.pallas_call(
        reduce_kernel,
        out_shape=[
            jax.ShapeDtypeStruct((8, 8, width), BF),
            jax.ShapeDtypeStruct((2, 8, 64, 128), BF),
            jax.ShapeDtypeStruct((2, 8, 8, 8, columns), BF),
        ],
        in_specs=[pl.BlockSpec(memory_space=pltpu.VMEM)] * 3,
        out_specs=[pl.BlockSpec(memory_space=pltpu.VMEM)] * 3,
        scratch_shapes=[
            pltpu.VMEM((8, 2, 4, 8, width), BF),
            pltpu.VMEM((4, 2, 8, 8, width), BF),
            pltpu.VMEM((3, 2, 8, 8, width), BF),
            pltpu.VMEM((2, 8, 8, width), BF),
            pltpu.VMEM((2, 8, 8, width), F32),
            pltpu.VMEM((8, 8, width), BF),
            pltpu.VMEM((8, 8, width), BF),
            pltpu.VMEM((8, 64, 128), BF),
            pltpu.VMEM((7, 8, width), BF),
            pltpu.VMEM((7, 64, 128), BF),
            dma, dma, dma((3,)), dma((3,)), dma, dma, dma((7,)), dma((7,)), dma((7,)), dma((7,)),
            dma((7,)), dma((7,)), dma((7,)), dma((7,)), dma((7,)), dma((7,)), dma((2,)), dma((2,)), dma,
        ],
        compiler_params=pltpu.CompilerParams(
            collective_id=1, has_side_effects=True, vmem_limit_bytes=20 * 2**20
        ),
    )(part, own, hidden)


def on_device(queries, out_grad, out_saved, logsumexp, parents, latents, hidden, latent_weight):
    tokens, heads, width = queries.shape
    rows = tokens * heads
    keys, qt, do, ld = gather(
        latents, logsumexp.T, queries.transpose(1, 2, 0),
        out_grad.reshape(rows, RANK), out_saved.reshape(rows, RANK),
    )
    query_grad, part, own = core_attn(parents, qt, do, ld, keys.reshape(-1, width))
    shape = (8, 2, 2, 4, 8, width)
    row_block, cols, hidden_all = reduce_and_spread(
        part.reshape(shape), own.reshape(shape), hidden.reshape(8, 8, -1)
    )
    core = lax.rem(lax.axis_index("ba"), 2)
    cols = lax.dynamic_slice_in_dim(cols.reshape(1024, 128), core * 36, 36, axis=1)
    weight_grad = lax.dot_general(
        cols, hidden_all.reshape(1024, -1), (((0,), (0,)), ((), ())), preferred_element_type=F32
    ).astype(BF)
    input_grad = jnp.dot(
        row_block.reshape(64, width), latent_weight, preferred_element_type=F32
    ).astype(BF)
    return query_grad.transpose(2, 0, 1), weight_grad, input_grad


def solution(mesh):
    return jax.shard_map(
        on_device,
        mesh=mesh,
        in_specs=(
            P("ba", "ha", None),
            P("ba", "ha", None),
            P("ba", "ha", None),
            P("ba", "ha"),
            P("ba"),
            P(("ba", "ha"), None),
            P("ba", "ha"),
            P(None, "ha"),
        ),
        out_specs=(P("ba", "ha", None), P("ba", "ha"), P("ba", "ha")),
        check_vma=False,
    )
```

time: 97.6 us -> 76.8 us (0.79); the launches traced: 95.8 us -> 77.1 us
  Pallas kernels: 80.8 us -> 71.1 us
  local copies, waits for them, and re-layouts: 10.5 us -> 3.15 us
  matrix products: 3.79 us -> 2.17 us
    pallas_call x1, Pallas kernels: 41.4 us -> 34.3 us  [reduce_and_spread(): pl.pallas_call(reduce_kernel, out_shape=[jax.ShapeDtypeStruct((8, 8, widt...]
    unnamed x9 -> x12, local copies, waits for them, and re-layouts: 9.76 us -> 3.15 us
    pallas_call x2, Pallas kernels: 39.4 us -> 36.8 us  [the longest x1 23.2 us: gather(): pl.pallas_call(gather_kernel, out_shape=[jax.ShapeDtypeStruct((2, 4, 2, 2...]
    dot_general x1, matrix products: 2.83 us -> 1.21 us  [on_device(): lax.dot_general(cols, hidden_all.reshape(1024, -1), (((0,), (0,)), ((), (...]
where the time goes in v2:
time: 76.8 us; the launch traced here: 77.1 us
  Pallas kernels  71.1 us (93%)
  local copies, waits for them, and re-layouts  3.15 us (4%)
  matrix products  2.17 us (3%)
    pallas_call x1, Pallas kernels, reduce_and_spread(): pl.pallas_call(reduce_kernel, out_shape=[jax.ShapeDtypeStruct((8, 8, widt...  34.3 us
    pallas_call x1, Pallas kernels, gather(): pl.pallas_call(gather_kernel, out_shape=[jax.ShapeDtypeStruct((2, 4, 2, 2...  23.2 us
    pallas_call x1, Pallas kernels, core_attn(): pl.pallas_call(attn_kernel, in_specs=[pl.BlockSpec(memory_space=pltpu.SME...  13.6 us
    unnamed x12, local copies, waits for them, and re-layouts  3.15 us

profile of v2, /device:TPU:1, one launch (start us, length us, event | category | flops | bytes accessed | tf_op | source)
XLA Modules:
  0.0 77.1 jit_solution(4340037402356019981)
XLA Ops:
  0.6 0.0 copy-start
  0.6 0.0 copy-start.3
  0.7 0.8 %copy-done.3 = bf16[8,576]{1,0:T(8,128)(2,1)S(1)} copy-done((bf16[8,576]{1,0:T(8,128)(2,1)S(1)}, bf16[8,576]{1,0:T(8,128)(2,1)}, u32[]{:S(2)}) %copy-start.3) | copy-done | bytes 9240
  1.4 0.0 copy-start.4
  1.4 0.7 copy-done.4
  2.1 0.0 copy-start.5
  2.1 23.2 %shard_map.103 = (bf16[2,4,2,2,4,8,576]{6,5,4,3,2,1,0:T(8,128)(2,1)S(1)}, bf16[8,576,256]{2,1,0:T(8,128)(2,1)}, bf16[8,256,512]{2,1,0:T(8,128)(2,1)S(1)}, f32[2,8,256]{2,1,0:T(8,128)S(1)}) custom-call(bf16[8,576]{1,0:T(8,128)(2,1)S(1)} %copy-done.3, f32[8,256]{1,0:T(8,128)S(1)} %bitcast.22, bf16[8,576,256]{2,1,0:T(8,128)(2,1)} %bitcast.23, ...), custom_call_target="tpu_custom_call" | custom-call | tf_op jit(solution)/shard_map/pallas_call | solution.py:215
  25.3 0.0 copy-done.5
  25.3 0.0 copy-start.1
  25.3 1.7 %copy-done.1 = bf16[8,576,256]{2,1,0:T(8,128)(2,1)S(1)} copy-done((bf16[8,576,256]{2,1,0:T(8,128)(2,1)S(1)}, bf16[8,576,256]{2,1,0:T(8,128)(2,1)}, u32[]{:S(2)}) %copy-start.1) | copy-done | bytes 2359320
  27.0 0.0 copy-start.2
  27.0 13.6 %shard_map.104 = (bf16[8,576,256]{2,1,0:T(8,128)(2,1)}, bf16[1024,576]{1,0:T(8,128)(2,1)S(1)}, f32[1024,576]{1,0:T(8,128)S(1)}) custom-call(s32[256]{0:T(256)S(1)} %copy-done.5, bf16[8,576,256]{2,1,0:T(8,128)(2,1)S(1)} %copy-done.1, bf16[8,256,512]{2,1,0:T(8,128)(2,1)S(1)} %get-tuple-element.14.do_ref, f32[2,8,256]{2,1,0:T(8,128)S(1)} %get-tuple-element.15.ld_ref, ...), custom_call_target="tpu_custom_call" | custom-call | tf_op jit(solution)/shard_map/pallas_call | solution.py:75
  40.6 0.0 copy-done.2
  40.6 34.3 %shard_map.105 = (bf16[8,8,576]{2,1,0:T(8,128)(2,1)S(1)}, bf16[2,8,64,128]{3,2,1,0:T(8,128)(2,1)S(1)}, bf16[2,8,8,8,896]{4,3,2,1,0:T(8,128)(2,1)S(1)}) custom-call(bf16[8,2,2,4,8,576]{5,4,3,2,1,0:T(8,128)(2,1)S(1)} %bitcast.18, f32[8,2,2,4,8,576]{5,4,3,2,1,0:T(8,128)S(1)} %bitcast.16, bf16[8,8,896]{2,1,0:T(8,128)(2,1)S(1)} %bitcast.21), custom_call_target="tpu_custom_call" | custom-call | tf_op jit(solution)/shard_map/pallas_call | solution.py:344
  74.9 1.2 %convolution_convert_fusion.1 = bf16[36,896]{1,0:T(8,128)(2,1)} fusion(bf16[1024,896]{1,0:T(8,128)(2,1)S(1)} %bitcast.17, bf16[1024,128]{1,0:T(8,128)(2,1)S(1)} %bitcast.20, s32[]{:T(128)S(6)} %select_n.3), kind=kOutput, calls=%fused_computation.1 | convolution fusion | flops 66092544 | bytes 2161668 | tf_op jit(solution)/shard_map/dot_general | solution.py:387
  76.1 0.0 copy-done
  76.1 1.0 %convolution_convert_fusion = bf16[64,896]{1,0:T(8,128)(2,1)} fusion(bf16[576,896]{1,0:T(8,128)(2,1)S(1)} %copy-done, bf16[8,8,576]{2,1,0:T(8,128)(2,1)S(1)} %get-tuple-element.22), kind=kOutput, calls=%fused_computation | convolution fusion | flops 66117632 | bytes 1220608 | tf_op jit(solution)/shard_map/dot_general | solution.py:390
Async XLA Ops:
  0.6 75.5 %copy-start = (bf16[576,896]{1,0:T(8,128)(2,1)S(1)}, bf16[576,896]{1,0:T(8,128)(2,1)}, u32[]{:S(2)}) copy-start(bf16[576,896]{1,0:T(8,128)(2,1)} %param.15) | copy-start | bytes 3096580
  0.6 0.8 %copy-start.3 = (bf16[8,576]{1,0:T(8,128)(2,1)S(1)}, bf16[8,576]{1,0:T(8,128)(2,1)}, u32[]{:S(2)}) copy-start(bf16[8,576]{1,0:T(8,128)(2,1)} %lat_ref.1) | copy-start | bytes 27652
  1.4 0.7 copy-start.4
  2.1 23.2 %copy-start.5 = (s32[256]{0:T(256)S(1)}, s32[256]{0:T(256)}, u32[]{:S(2)}) copy-start(s32[256]{0:T(256)} %par_ref.1) | copy-start | bytes 3076
  25.3 1.7 %copy-start.1 = (bf16[8,576,256]{2,1,0:T(8,128)(2,1)S(1)}, bf16[8,576,256]{2,1,0:T(8,128)(2,1)}, u32[]{:S(2)}) copy-start(bf16[8,576,256]{2,1,0:T(8,128)(2,1)} %get-tuple-element.13.qt_ref) | copy-start | bytes 7077892
  27.0 13.6 %copy-start.2 = (bf16[64,896]{1,0:T(8,128)(2,1)S(1)}, bf16[64,896]{1,0:T(8,128)(2,1)}, u32[]{:S(2)}) copy-start(bf16[64,896]{1,0:T(8,128)(2,1)} %param.14) | copy-start | bytes 344068

commit v3 on v2

--- a/solution.py
+++ b/solution.py
@@ -14,11 +14,15 @@
 F32 = jnp.float32
 BF = jnp.bfloat16
 
-def attn_kernel(par_ref, qt_ref, do_ref, ld_ref, k_ref, dq_ref, part_ref, acc_ref, kt_ref, dqt_ref, p0, d0, p1, d1):
+def attn_kernel(par_ref, qt_ref, do_ref, delta_ref, lse_in, k_ref, dq_ref, part_ref, acc_ref, kt_ref, dqt_ref, lse_ref, p0, d0, p1, d1):
     nb = qt_ref.shape[0]
     keys = k_ref.shape[0]
     per = par_ref.shape[0] // nb
     acc_ref[...] = jnp.zeros_like(acc_ref)
+    run = lse_in.shape[1] // nb
+    for b in range(nb):
+        lanes = slice(b * run, (b + 1) * run)
+        lse_ref[b:b + 1, :] = jnp.concatenate([lse_in[h:h + 1, lanes] for h in range(nb)], axis=1)
     p1[...] = jnp.zeros_like(p1)
     d1[...] = jnp.zeros_like(d1)
     for i in range(keys // KT):
@@ -34,16 +38,16 @@
         s = lax.dot_general(k_ref[pl.ds(at, KT), :], qt_ref[bb], NN, preferred_element_type=F32)
         g = lax.dot_general(k_ref[pl.ds(at, KT), :RANK], do_ref[bb], NT, preferred_element_type=F32)
         idx = at + lax.broadcasted_iota(jnp.int32, (KT, 1), 0)
-        p = jnp.where(idx <= limit, jnp.exp(s * SCALE - ld_ref[0, pl.ds(bb, 1), :]), 0.0)
-        d_out[...] = (p * (g * SCALE - ld_ref[1, pl.ds(bb, 1), :])).astype(BF)
+        p = jnp.where(idx <= limit, jnp.exp(s * SCALE - lse_ref[pl.ds(bb, 1), :]), 0.0)
+        d_out[...] = (p * (g - delta_ref[pl.ds(bb, 1), :])).astype(BF)
         p_out[...] = p.astype(BF)
 
         oat = pl.multiple_of(ot * KT, KT)
         ds, pp = d_in[...], p_in[...]
         key = lax.dot_general(ds, qt_ref[ob], NT, preferred_element_type=F32)
         val = lax.dot_general(pp, do_ref[ob], NN, preferred_element_type=F32)
-        acc_ref[pl.ds(oat, KT), :RANK] += key[:, :RANK] + val
-        acc_ref[pl.ds(oat, KT), RANK:] += key[:, RANK:]
+        acc_ref[pl.ds(oat, KT), :RANK] += key[:, :RANK] * SCALE + val
+        acc_ref[pl.ds(oat, KT), RANK:] += key[:, RANK:] * SCALE
         dq = lax.dot_general(kt_ref[:, pl.ds(oat, KT)], ds, NN, preferred_element_type=F32)
         dqt_ref[ob] = dq + jnp.where(fresh, 0.0, dqt_ref[ob])
         more = (t + 1) * KT <= limit
@@ -61,24 +65,25 @@
     lax.fori_loop(0, (steps + 1) // 2, trip, (0, 0, 0, 0, False))
 
     for b in range(nb):
-        block = dqt_ref[b].astype(BF)
+        block = (dqt_ref[b] * SCALE).astype(BF)
         width = block.shape[1] // nb
         for h in range(nb):
             dq_ref[h, :, b * width:(b + 1) * width] = block[:, h * width:(h + 1) * width]
     part_ref[...] = acc_ref[...].astype(BF)
 
 
-def core_attn(parents, qt, do, ld, k):
+def core_attn(parents, qt, do, delta, lse, k):
     nb, width, rb = qt.shape
     keys = k.shape[0]
     vm = pl.BlockSpec(memory_space=pltpu.VMEM)
     return pl.pallas_call(
         attn_kernel,
-        in_specs=[pl.BlockSpec(memory_space=pltpu.SMEM)] + [vm] * 4,
+        in_specs=[pl.BlockSpec(memory_space=pltpu.SMEM)] + [vm] * 5,
         out_specs=[vm] * 3,
         scratch_shapes=[
             pltpu.VMEM((width, keys), BF),
             pltpu.VMEM((nb, width, rb), F32),
+            pltpu.VMEM((nb, rb), F32),
         ] + [pltpu.VMEM((KT, rb), BF)] * 4,
         out_shape=[
             jax.ShapeDtypeStruct((nb, width, rb), BF),
@@ -86,7 +91,7 @@
             jax.ShapeDtypeStruct((keys, width), F32),
         ],
         compiler_params=pltpu.CompilerParams(vmem_limit_bytes=32 * 2**20),
-    )(parents, qt, do, ld, k)
+    )(parents, qt, do, delta, lse, k)
 
 def place():
     ba, ha = lax.axis_index("ba"), lax.axis_index("ha")
@@ -116,8 +121,8 @@
     )
 
 
-def prepare(b, perm, q_in, do_in, os_in, lse_ref, qt_ref, do_ref, ld_ref):
-    heads, tokens = lse_ref.shape
+def prepare(b, perm, q_in, do_in, os_in, qt_ref, do_ref, delta_ref):
+    heads, _, tokens = q_in.shape
     run = tokens // heads
     lanes = slice(b * run, (b + 1) * run)
     qt_ref[b] = jnp.concatenate([q_in[h, :, lanes] for h in range(heads)], axis=1)
@@ -129,11 +134,10 @@
     part = prod[:, 0:128]
     for i in range(1, RANK // 128):
         part = part + prod[:, i * 128:(i + 1) * 128]
-    ld_ref[0, b:b + 1, :] = jnp.concatenate([lse_ref[h:h + 1, lanes] for h in range(heads)], axis=1)
-    ld_ref[1, b:b + 1, :] = jnp.sum(part.T, axis=0, keepdims=True) * SCALE
-
-
-def gather_kernel(lat_ref, lse_ref, q_hbm, do_hbm, os_hbm, out_ref, qt_ref, do_ref, ld_ref,
+    delta_ref[b:b + 1, :] = jnp.sum(part.T, axis=0, keepdims=True)
+
+
+def gather_kernel(lat_ref, q_hbm, do_hbm, os_hbm, out_ref, qt_ref, do_ref, delta_ref,
                   q_in, do_in, os_in, plane_s, plane_r, line_s, line_r, pair_s, pair_r, load_s):
     loads = [
         pltpu.make_async_copy(src, dst, load_s.at[n])
@@ -151,64 +155,84 @@
         return device(core, jnp.where(first, pu, pw), lax.rem(y + dy, 4), jnp.where(first, pw, pu))
 
     partner = device(1 - core, x, y, z)
-    plane = [(du, dy) for dy in range(4) for du in range(4) if du or dy]
-    plane.sort(key=lambda d: -(min(d[0], 4 - d[0]) + min(d[1], 4 - d[1])))
+    plane = [(du, dy) for dy in (2, 1, 3, 0) for du in (2, 1, 3, 0) if du or dy]
     meet([at(du, dy, 0) for du, dy in plane] + [at(0, 0, dw) for dw in (1, 2, 3)] + [partner])
     mine = out_ref.at[ylo, z, core, yhi, x]
-    copies = []
+    copies = {}
     for n, (du, dy) in enumerate(plane):
         copy = send(lat_ref, mine, plane_s.at[n], plane_r.at[n], at(du, dy, 0))
         copy.start()
-        copies.append(copy)
+        copies[du, dy] = copy
     out_ref[ylo, z, core, yhi, x] = lat_ref[...]
     for load in loads:
         load.wait()
-    heads, tokens = lse_ref.shape
+    heads, _, tokens = q_in.shape
     row = lax.broadcasted_iota(jnp.int32, (tokens, tokens), 0)
     col = lax.broadcasted_iota(jnp.int32, (tokens, tokens), 1)
     run = tokens // heads
     perm = jnp.where(col == lax.rem(row, run) * heads + row // run, 1.0, 0.0).astype(BF)
-    for b in range(heads // 2):
-        prepare(b, perm, q_in, do_in, os_in, lse_ref, qt_ref, do_ref, ld_ref)
-    for copy in copies:
-        copy.wait_recv()
-
-    def block(c, k):
-        return out_ref.at[:, k, 0] if c == 0 else out_ref.at[:, :, 1, :, k]
-
-    def line_copy(c, n, dw):
-        return send(block(c, w), block(c, w), line_s.at[n], line_r.at[n], at(0, 0, dw))
-
-    def pair_copy(c, n, k):
-        return send(block(c, k), block(c, k), pair_s.at[n], pair_r.at[n], partner)
-
-    lines = ((2, 1, 3))
+
+    def ready(lo, hi):
+        for b in range(lo, hi):
+            prepare(b, perm, q_in, do_in, os_in, qt_ref, do_ref, delta_ref)
+
+    def block(c, k, dy):
+        row_y = lax.rem(y + 4 - dy, 4)
+        hi, lo = row_y // 2, lax.rem(row_y, 2)
+        return out_ref.at[lo, k, 0, hi] if c == 0 else out_ref.at[lo, :, 1, hi, k]
+
+    def line_copy(c, dw, dy, k, hop):
+        n = (dw - 1) * 4 + dy
+        return send(block(c, k, dy), block(c, k, dy), line_s.at[n], line_r.at[n], at(0, 0, hop))
+
+    def pair_copy(c, dw, dy):
+        n, k = dw * 4 + dy, lax.rem(w + 4 - dw, 4)
+        return send(block(c, k, dy), block(c, k, dy), pair_s.at[n], pair_r.at[n], partner)
+
+    order, relayed = (0, 1, 3, 2), (0, 1)
+    ready(0, 2)
+    for dy in order:
+        for du in (0, 1, 3, 2):
+            if du or dy:
+                copies[du, dy].wait_recv()
+        for c in (0, 1):
+            @pl.when(core == c)
+            def _():
+                for dw in (1, 3) if dy in relayed else (2, 1, 3):
+                    line_copy(c, dw, dy, w, dw).start()
+                pair_copy(c, 0, dy).start()
+    ready(2, 4)
     for c in (0, 1):
         @pl.when(core == c)
         def _():
-            for n, dw in enumerate(lines):
-                line_copy(c, n, dw).start()
-            pair_copy(c, 3, w).start()
-
-    for b in range(heads // 2, heads):
-        prepare(b, perm, q_in, do_in, os_in, lse_ref, qt_ref, do_ref, ld_ref)
-
+            for dy in relayed:
+                line_copy(c, 3, dy, w, 3).wait_recv()
+                line_copy(c, 2, dy, lax.rem(w + 1, 4), 3).start()
+                pair_copy(c, 3, dy).start()
+    ready(4, heads)
     for c in (0, 1):
         @pl.when(core == c)
         def _():
-            for n, dw in ((1, 1), (2, 3), (0, 2)):
-                line_copy(c, n, dw).wait_recv()
-                pair_copy(c, n, lax.rem(w + 4 - dw, 4)).start()
-            for n, dw in enumerate(lines):
-                line_copy(c, n, dw).wait_send()
-            for n in range(4):
-                pair_copy(c, n, w).wait()
-
-    for copy in copies:
+            for dy in order:
+                for dw in (1, 3):
+                    if dw == 3 and dy in relayed:
+                        continue
+                    line_copy(c, dw, dy, w, dw).wait_recv()
+                    pair_copy(c, dw, dy).start()
+            for dy in order:
+                line_copy(c, 2, dy, w, 2).wait_recv()
+                pair_copy(c, 2, dy).start()
+            for dy in order:
+                for dw in (1, 2, 3):
+                    line_copy(c, dw, dy, w, dw).wait_send()
+                for dw in range(4):
+                    pair_copy(c, dw, dy).wait()
+
+    for copy in copies.values():
         copy.wait_send()
 
 
-def gather(latents, lse, q, do, osv):
+def gather(latents, q, do, osv):
     rows, width = latents.shape
     heads, _, tokens = q.shape
     vm, hbm = pl.BlockSpec(memory_space=pltpu.VMEM), pl.BlockSpec(memory_space=pltpu.HBM)
@@ -218,16 +242,16 @@
             jax.ShapeDtypeStruct((2, 4, 2, 2, 4, rows, width), BF),
             jax.ShapeDtypeStruct((heads, width, tokens), BF),
             jax.ShapeDtypeStruct((heads, tokens, RANK), BF),
-            jax.ShapeDtypeStruct((2, heads, tokens), F32),
+            jax.ShapeDtypeStruct((heads, tokens), F32),
         ],
-        in_specs=[vm, vm, hbm, hbm, hbm],
+        in_specs=[vm, hbm, hbm, hbm],
         out_specs=[vm] * 4,
         scratch_shapes=[pltpu.VMEM(a.shape, BF) for a in (q, do, osv)]
-        + [pltpu.SemaphoreType.DMA((n,)) for n in (15, 15, 3, 3, 4, 4, 3)],
+        + [pltpu.SemaphoreType.DMA((n,)) for n in (15, 15, 12, 12, 16, 16, 3)],
         compiler_params=pltpu.CompilerParams(
             collective_id=0, has_side_effects=True, vmem_limit_bytes=50 * 2**20
         ),
-    )(latents, lse, q, do, osv)
+    )(latents, q, do, osv)
 
 
 def total(*blocks):
@@ -238,7 +262,7 @@
 
 
 def reduce_kernel(part_ref, own_ref, hid_ref, rows_ref, cols_ref, hall_ref,
-                  got0, acc0, got1, acc1, keep1, got2, acc2, colbuf, gotr, gotc,
+                  got0, acc0, got1, fwd, acc1, keep1, got2, acc2, colbuf, gotr, gotc,
                   s0, r0, s1, r1, s2, r2, s3, r3, s3c, r3c, s4, r4, s4c, r4c, sh, rh, sp, rp, lsem):
     core, x, yhi, ylo, z = place()
     y = yhi * 2 + ylo
@@ -259,12 +283,17 @@
 
     meet([partner] + [head_at(*d)[1] for d in heads] + [chip_at(*d)[1] for d in chips])
 
-    pending = []
+    opp, right, left = lax.rem(x + 2, 4), lax.rem(x + 1, 4), lax.rem(x + 3, 4)
+    chunks = (opp, right, left, x)
+
+    def swap_copy(c, n):
+        return send(part_ref.at[:, 1 - c, :, chunks[n]], got0.at[n], s0.at[n], r0.at[n], partner)
+
     for c in (0, 1):
         @pl.when(core == c)
         def _():
-            send(part_ref.at[:, 1 - c], got0, s0, r0, partner).start()
-    first = send(part_ref.at[:, 0], got0, s0, r0, partner)
+            for n in range(4):
+                swap_copy(c, n).start()
     own_hidden = pltpu.make_async_copy(hid_ref, hall_ref.at[core, :, g], lsem)
     own_hidden.start()
     hidden = []
@@ -272,26 +301,46 @@
         copy = send(hid_ref, hall_ref.at[core, :, g], sh.at[n], rh.at[n], chip_at(*d)[1])
         copy.start()
         hidden.append(copy)
-    first.wait_recv()
-
-    for px in range(4):
-        for py in range(2):
-            acc0[px, py] = total(own_ref[:, core, py, px], got0[:, py, px]).astype(BF)
-
-    line = []
-    for n, dx in enumerate((2, 1, 3)):
-        to, peer = head_at(0, dx)
-        copy = send(acc0.at[to - yhi * 4], got1.at[n], s1.at[n], r1.at[n], peer)
-        copy.start()
-        line.append(copy)
-    for copy in line:
-        copy.wait_recv()
+    def paired(n, py):
+        return total(own_ref[:, core, py, chunks[n]], got0[n, :, py])
+
+    def line_copy(n, src, dst, dx):
+        return send(src, dst, s1.at[n], r1.at[n], head_at(0, dx)[1])
+
+    line = [
+        line_copy(0, acc0.at[1, 0], got1.at[0, 0], 1),
+        line_copy(1, acc0.at[1, 1], got1.at[0, 1], 1),
+        line_copy(2, acc0.at[2, 0], got1.at[1, 0], 3),
+        line_copy(3, acc0.at[2, 1], got1.at[1, 1], 3),
+        line_copy(4, acc0.at[0, 0], fwd.at[0], 1),
+        line_copy(5, acc0.at[0, 1], fwd.at[1], 3),
+    ]
+    swap_copy(0, 0).wait_recv()
+    acc0[0, 0] = paired(0, 0).astype(BF)
+    line[4].start()
+    acc0[0, 1] = paired(0, 1).astype(BF)
+    line[5].start()
+    swap_copy(0, 1).wait_recv()
+    acc0[1, 1] = paired(1, 1).astype(BF)
+    line[1].start()
+    swap_copy(0, 2).wait_recv()
+    acc0[2, 0] = paired(2, 0).astype(BF)
+    line[2].start()
+    swap_copy(0, 3).wait_recv()
     for py in range(2):
-        summed = total(own_ref[:, core, py, x], got0[:, py, x], got1[0, py], got1[1, py], got1[2, py])
-        keep1[py] = summed
-        acc1[py] = summed.astype(BF)
-    other = send(acc1.at[1 - yhi], got2, s2, r2, head_at(1, 0)[1])
+        keep1[py] = paired(3, py)
+    line[4].wait_recv()
+    acc0[1, 0] = (paired(1, 0) + fwd[0].astype(F32)).astype(BF)
+    line[0].start()
+    line[5].wait_recv()
+    acc0[2, 1] = (paired(2, 1) + fwd[1].astype(F32)).astype(BF)
+    line[3].start()
+    for n in range(4):
+        line[n].wait_recv()
+    acc1[...] = total(keep1[1 - yhi], got1[0, 1 - yhi], got1[1, 1 - yhi]).astype(BF)
+    other = send(acc1, got2, s2, r2, head_at(1, 0)[1])
     other.start()
+    keep1[yhi] = total(keep1[yhi], got1[0, yhi], got1[1, yhi])
     other.wait_recv()
     summed = total(keep1[yhi], got2[...])
     keep1[0] = summed
@@ -331,7 +380,8 @@
         copy.wait_recv()
     last = send(cols_ref.at[core], cols_ref.at[core], sp.at[1], rp.at[1], partner)
     last.start()
-    first.wait_send()
+    for n in range(4):
+        swap_copy(0, n).wait_send()
     for copy in hidden + line + [other] + rows + cols + spread:
         copy.wait_send()
     swap.wait()
@@ -351,17 +401,18 @@
         in_specs=[pl.BlockSpec(memory_space=pltpu.VMEM)] * 3,
         out_specs=[pl.BlockSpec(memory_space=pltpu.VMEM)] * 3,
         scratch_shapes=[
-            pltpu.VMEM((8, 2, 4, 8, width), BF),
-            pltpu.VMEM((4, 2, 8, 8, width), BF),
+            pltpu.VMEM((4, 8, 2, 8, width), BF),
             pltpu.VMEM((3, 2, 8, 8, width), BF),
+            pltpu.VMEM((2, 2, 8, 8, width), BF),
             pltpu.VMEM((2, 8, 8, width), BF),
+            pltpu.VMEM((8, 8, width), BF),
             pltpu.VMEM((2, 8, 8, width), F32),
             pltpu.VMEM((8, 8, width), BF),
             pltpu.VMEM((8, 8, width), BF),
             pltpu.VMEM((8, 64, 128), BF),
             pltpu.VMEM((7, 8, width), BF),
             pltpu.VMEM((7, 64, 128), BF),
-            dma, dma, dma((3,)), dma((3,)), dma, dma, dma((7,)), dma((7,)), dma((7,)), dma((7,)),
+            dma((4,)), dma((4,)), dma((6,)), dma((6,)), dma, dma, dma((7,)), dma((7,)), dma((7,)), dma((7,)),
             dma((7,)), dma((7,)), dma((7,)), dma((7,)), dma((7,)), dma((7,)), dma((2,)), dma((2,)), dma,
         ],
         compiler_params=pltpu.CompilerParams(
@@ -373,11 +424,13 @@
 def on_device(queries, out_grad, out_saved, logsumexp, parents, latents, hidden, latent_weight):
     tokens, heads, width = queries.shape
     rows = tokens * heads
-    keys, qt, do, ld = gather(
-        latents, logsumexp.T, queries.transpose(1, 2, 0),
+    keys, qt, do, delta = gather(
+        latents, queries.transpose(1, 2, 0),
         out_grad.reshape(rows, RANK), out_saved.reshape(rows, RANK),
     )
-    query_grad, part, own = core_attn(parents, qt, do, ld, keys.reshape(-1, width))
+    query_grad, part, own = core_attn(
+        parents, qt, do, delta, logsumexp.T, keys.reshape(-1, width)
+    )
     shape = (8, 2, 2, 4, 8, width)
     row_block, cols, hidden_all = reduce_and_spread(
         part.reshape(shape), own.reshape(shape), hidden.reshape(8, 8, -1)

time: 76.8 us -> 77.9 us (1.014); the launches traced: 77.1 us -> 77.1 us
    pallas_call x1, Pallas kernels: 34.3 us -> 35.7 us  [reduce_and_spread(): pl.pallas_call(reduce_kernel, out_shape=[jax.ShapeDtypeStruct((8, 8, widt...]
    pallas_call x1, Pallas kernels: 23.2 us -> 22.2 us  [gather(): pl.pallas_call(gather_kernel, out_shape=[jax.ShapeDtypeStruct((2, 4, 2, 2...]
where the time goes in v3:
time: 77.9 us; the launch traced here: 77.1 us
  Pallas kernels  71.7 us (92%)
  local copies, waits for them, and re-layouts  2.46 us (3%)
  matrix products  2.17 us (3%)
    pallas_call x1, Pallas kernels, reduce_and_spread(): pl.pallas_call(reduce_kernel, out_shape=[jax.ShapeDtypeStruct((8, 8, widt...  35.7 us
    pallas_call x1, Pallas kernels, gather(): pl.pallas_call(gather_kernel, out_shape=[jax.ShapeDtypeStruct((2, 4, 2, 2...  22.2 us
    pallas_call x1, Pallas kernels, core_attn(): pl.pallas_call(attn_kernel, in_specs=[pl.BlockSpec(memory_space=pltpu.SME...  13.8 us
    unnamed x12, local copies, waits for them, and re-layouts  2.46 us

profile of v3, /device:TPU:1, one launch (start us, length us, event | category | flops | bytes accessed | tf_op | source)
XLA Modules:
  0.0 77.1 jit_solution(15438643996878826769)
XLA Ops:
  0.6 0.0 copy-start
  0.6 0.0 copy-start.3
  0.7 0.8 %copy-done.3 = bf16[8,576]{1,0:T(8,128)(2,1)S(1)} copy-done((bf16[8,576]{1,0:T(8,128)(2,1)S(1)}, bf16[8,576]{1,0:T(8,128)(2,1)}, u32[]{:S(2)}) %copy-start.3) | copy-done | bytes 9240
  1.4 0.0 copy-start.4
  1.4 0.0 copy-start.5
  1.4 22.2 %shard_map.103 = (bf16[2,4,2,2,4,8,576]{6,5,4,3,2,1,0:T(8,128)(2,1)S(1)}, bf16[8,576,256]{2,1,0:T(8,128)(2,1)}, bf16[8,256,512]{2,1,0:T(8,128)(2,1)S(1)}, f32[8,256]{1,0:T(8,128)S(1)}) custom-call(bf16[8,576]{1,0:T(8,128)(2,1)S(1)} %copy-done.3, bf16[8,576,256]{2,1,0:T(8,128)(2,1)} %bitcast.23, bf16[2048,512]{1,0:T(8,128)(2,1)} %bitcast.24, ...), custom_call_target="tpu_custom_call" | custom-call | tf_op jit(solution)/shard_map/pallas_call | solution.py:239
  23.6 0.0 copy-done.4
  23.6 0.0 copy-done.5
  23.6 0.0 copy-start.1
  23.6 1.7 %copy-done.1 = bf16[8,576,256]{2,1,0:T(8,128)(2,1)S(1)} copy-done((bf16[8,576,256]{2,1,0:T(8,128)(2,1)S(1)}, bf16[8,576,256]{2,1,0:T(8,128)(2,1)}, u32[]{:S(2)}) %copy-start.1) | copy-done | bytes 2359320
  25.3 0.0 copy-start.2
  25.3 13.8 %shard_map.104 = (bf16[8,576,256]{2,1,0:T(8,128)(2,1)}, bf16[1024,576]{1,0:T(8,128)(2,1)S(1)}, f32[1024,576]{1,0:T(8,128)S(1)}) custom-call(s32[256]{0:T(256)S(1)} %copy-done.5, bf16[8,576,256]{2,1,0:T(8,128)(2,1)S(1)} %copy-done.1, bf16[8,256,512]{2,1,0:T(8,128)(2,1)S(1)} %get-tuple-element.14.do_ref, f32[8,256]{1,0:T(8,128)S(1)} %get-tuple-element.15.delta_ref, ...), custom_call_target="tpu_custom_call" | custom-call | tf_op jit(solution)/shard_map/pallas_call | solution.py:79
  39.1 0.0 copy-done.2
  39.1 35.7 %shard_map.105 = (bf16[8,8,576]{2,1,0:T(8,128)(2,1)S(1)}, bf16[2,8,64,128]{3,2,1,0:T(8,128)(2,1)S(1)}, bf16[2,8,8,8,896]{4,3,2,1,0:T(8,128)(2,1)S(1)}) custom-call(bf16[8,2,2,4,8,576]{5,4,3,2,1,0:T(8,128)(2,1)S(1)} %bitcast.18, f32[8,2,2,4,8,576]{5,4,3,2,1,0:T(8,128)S(1)} %bitcast.16, bf16[8,8,896]{2,1,0:T(8,128)(2,1)S(1)} %bitcast.21), custom_call_target="tpu_custom_call" | custom-call | tf_op jit(solution)/shard_map/pallas_call | solution.py:394
  74.9 1.2 %convolution_convert_fusion.1 = bf16[36,896]{1,0:T(8,128)(2,1)} fusion(bf16[1024,896]{1,0:T(8,128)(2,1)S(1)} %bitcast.17, bf16[1024,128]{1,0:T(8,128)(2,1)S(1)} %bitcast.20, s32[]{:T(128)S(6)} %select_n.3), kind=kOutput, calls=%fused_computation.1 | convolution fusion | flops 66092544 | bytes 2161668 | tf_op jit(solution)/shard_map/dot_general | solution.py:440
  76.1 0.0 copy-done
  76.1 1.0 %convolution_convert_fusion = bf16[64,896]{1,0:T(8,128)(2,1)} fusion(bf16[576,896]{1,0:T(8,128)(2,1)S(1)} %copy-done, bf16[8,8,576]{2,1,0:T(8,128)(2,1)S(1)} %get-tuple-element.22), kind=kOutput, calls=%fused_computation | convolution fusion | flops 66117632 | bytes 1220608 | tf_op jit(solution)/shard_map/dot_general | solution.py:443
Async XLA Ops:
  0.6 75.5 %copy-start = (bf16[576,896]{1,0:T(8,128)(2,1)S(1)}, bf16[576,896]{1,0:T(8,128)(2,1)}, u32[]{:S(2)}) copy-start(bf16[576,896]{1,0:T(8,128)(2,1)} %param.15) | copy-start | bytes 3096580
  0.6 0.8 %copy-start.3 = (bf16[8,576]{1,0:T(8,128)(2,1)S(1)}, bf16[8,576]{1,0:T(8,128)(2,1)}, u32[]{:S(2)}) copy-start(bf16[8,576]{1,0:T(8,128)(2,1)} %lat_ref.1) | copy-start | bytes 27652
  1.4 22.2 %copy-start.4 = (f32[256,8]{0,1:T(8,128)S(1)}, f32[256,8]{0,1:T(8,128)}, u32[]{:S(2)}) copy-start(f32[256,8]{0,1:T(8,128)} %param.11) | copy-start | bytes 24580
  1.4 22.2 %copy-start.5 = (s32[256]{0:T(256)S(1)}, s32[256]{0:T(256)}, u32[]{:S(2)}) copy-start(s32[256]{0:T(256)} %par_ref.1) | copy-start | bytes 3076
  23.6 1.7 %copy-start.1 = (bf16[8,576,256]{2,1,0:T(8,128)(2,1)S(1)}, bf16[8,576,256]{2,1,0:T(8,128)(2,1)}, u32[]{:S(2)}) copy-start(bf16[8,576,256]{2,1,0:T(8,128)(2,1)} %get-tuple-element.13.qt_ref) | copy-start | bytes 7077892
  25.3 13.8 %copy-start.2 = (bf16[64,896]{1,0:T(8,128)(2,1)S(1)}, bf16[64,896]{1,0:T(8,128)(2,1)}, u32[]{:S(2)}) copy-start(bf16[64,896]{1,0:T(8,128)(2,1)} %param.14) | copy-start | bytes 344068

commit v4 on v3

--- a/solution.py
+++ b/solution.py
@@ -14,8 +14,10 @@
 F32 = jnp.float32
 BF = jnp.bfloat16
 
-def attn_kernel(par_ref, qt_ref, do_ref, delta_ref, lse_in, k_ref, dq_ref, part_ref, acc_ref, kt_ref, dqt_ref, lse_ref, p0, d0, p1, d1):
+def attn_kernel(par_ref, qt_hbm, do_ref, delta_ref, lse_in, k_ref, dq_hbm, part_ref, own_ref, acc_ref, kt_ref, dqt_ref, lse_ref, qt_ref, dq_ref, p0, d0, p1, d1, load_s, out_s):
     nb = qt_ref.shape[0]
+    for b in range(nb):
+        pltpu.make_async_copy(qt_hbm.at[b], qt_ref.at[b], load_s.at[b]).start()
     keys = k_ref.shape[0]
     per = par_ref.shape[0] // nb
     acc_ref[...] = jnp.zeros_like(acc_ref)
@@ -59,38 +61,55 @@
         carry = step(*carry, p1, d1, p0, d0)
         return step(*carry, p0, d0, p1, d1)
 
+    for b in range(nb):
+        pltpu.make_async_copy(qt_hbm.at[b], qt_ref.at[b], load_s.at[b]).wait()
     steps = 1
     for b in range(nb):
         steps = steps + par_ref[b * per] // KT + 1
     lax.fori_loop(0, (steps + 1) // 2, trip, (0, 0, 0, 0, False))
 
+    run = dq_ref.shape[2] // nb
     for b in range(nb):
         block = (dqt_ref[b] * SCALE).astype(BF)
-        width = block.shape[1] // nb
         for h in range(nb):
-            dq_ref[h, :, b * width:(b + 1) * width] = block[:, h * width:(h + 1) * width]
-    part_ref[...] = acc_ref[...].astype(BF)
+            dq_ref[h, :, b * run:(b + 1) * run] = block[:, h * run:(h + 1) * run]
+        if b == nb // 2 - 1 or b == nb - 1:
+            half = b // (nb // 2)
+            lanes = slice(half * 128, half * 128 + 128)
+            pltpu.make_async_copy(dq_ref.at[:, :, lanes], dq_hbm.at[:, :, lanes], out_s.at[half]).start()
+    core = lax.rem(lax.axis_index("ba"), 2)
+    for g in range(8):
+        mine = pl.multiple_of(g * 128 + core * 64, 64)
+        other = pl.multiple_of(g * 128 + (1 - core) * 64, 64)
+        part_ref[g] = acc_ref[pl.ds(other, 64), :].astype(BF)
+        own_ref[g] = acc_ref[pl.ds(mine, 64), :]
+    for half in range(2):
+        lanes = slice(half * 128, half * 128 + 128)
+        pltpu.make_async_copy(dq_ref.at[:, :, lanes], dq_hbm.at[:, :, lanes], out_s.at[half]).wait()
 
 
 def core_attn(parents, qt, do, delta, lse, k):
     nb, width, rb = qt.shape
     keys = k.shape[0]
-    vm = pl.BlockSpec(memory_space=pltpu.VMEM)
+    vm, hbm = pl.BlockSpec(memory_space=pltpu.VMEM), pl.BlockSpec(memory_space=pltpu.HBM)
     return pl.pallas_call(
         attn_kernel,
-        in_specs=[pl.BlockSpec(memory_space=pltpu.SMEM)] + [vm] * 5,
-        out_specs=[vm] * 3,
+        in_specs=[pl.BlockSpec(memory_space=pltpu.SMEM), hbm] + [vm] * 4,
+        out_specs=[hbm, vm, vm],
         scratch_shapes=[
+            pltpu.VMEM((keys, width), F32),
             pltpu.VMEM((width, keys), BF),
             pltpu.VMEM((nb, width, rb), F32),
             pltpu.VMEM((nb, rb), F32),
-        ] + [pltpu.VMEM((KT, rb), BF)] * 4,
+            pltpu.VMEM((nb, width, rb), BF),
+            pltpu.VMEM((nb, width, rb), BF),
+        ] + [pltpu.VMEM((KT, rb), BF)] * 4 + [pltpu.SemaphoreType.DMA((8,)), pltpu.SemaphoreType.DMA((2,))],
         out_shape=[
             jax.ShapeDtypeStruct((nb, width, rb), BF),
-            jax.ShapeDtypeStruct((keys, width), BF),
-            jax.ShapeDtypeStruct((keys, width), F32),
+            jax.ShapeDtypeStruct((8, keys // 16, width), BF),
+            jax.ShapeDtypeStruct((8, keys // 16, width), F32),
         ],
-        compiler_params=pltpu.CompilerParams(vmem_limit_bytes=32 * 2**20),
+        compiler_params=pltpu.CompilerParams(vmem_limit_bytes=48 * 2**20),
     )(parents, qt, do, delta, lse, k)
 
 def place():
@@ -138,7 +157,7 @@
 
 
 def gather_kernel(lat_ref, q_hbm, do_hbm, os_hbm, out_ref, qt_ref, do_ref, delta_ref,
-                  q_in, do_in, os_in, plane_s, plane_r, line_s, line_r, pair_s, pair_r, load_s):
+                  q_in, do_in, os_in, qt_s, plane_s, plane_r, line_s, line_r, pair_s, pair_r, load_s, out_s):
     loads = [
         pltpu.make_async_copy(src, dst, load_s.at[n])
         for n, (src, dst) in enumerate(((q_hbm, q_in), (do_hbm, do_in), (os_hbm, os_in)))
@@ -155,7 +174,7 @@
         return device(core, jnp.where(first, pu, pw), lax.rem(y + dy, 4), jnp.where(first, pw, pu))
 
     partner = device(1 - core, x, y, z)
-    plane = [(du, dy) for dy in (2, 1, 3, 0) for du in (2, 1, 3, 0) if du or dy]
+    plane = [(du, dy) for dy in (0, 2, 1, 3) for du in (2, 1, 3, 0) if du or dy]
     meet([at(du, dy, 0) for du, dy in plane] + [at(0, 0, dw) for dw in (1, 2, 3)] + [partner])
     mine = out_ref.at[ylo, z, core, yhi, x]
     copies = {}
@@ -174,7 +193,8 @@
 
     def ready(lo, hi):
         for b in range(lo, hi):
-            prepare(b, perm, q_in, do_in, os_in, qt_ref, do_ref, delta_ref)
+            prepare(b, perm, q_in, do_in, os_in, qt_s, do_ref, delta_ref)
+            pltpu.make_async_copy(qt_s.at[b], qt_ref.at[b], out_s.at[b]).start()
 
     def block(c, k, dy):
         row_y = lax.rem(y + 4 - dy, 4)
@@ -230,6 +250,8 @@
 
     for copy in copies.values():
         copy.wait_send()
+    for b in range(heads):
+        pltpu.make_async_copy(qt_s.at[b], qt_ref.at[b], out_s.at[b]).wait()
 
 
 def gather(latents, q, do, osv):
@@ -245,9 +267,9 @@
             jax.ShapeDtypeStruct((heads, tokens), F32),
         ],
         in_specs=[vm, hbm, hbm, hbm],
-        out_specs=[vm] * 4,
-        scratch_shapes=[pltpu.VMEM(a.shape, BF) for a in (q, do, osv)]
-        + [pltpu.SemaphoreType.DMA((n,)) for n in (15, 15, 12, 12, 16, 16, 3)],
+        out_specs=[vm, hbm, vm, vm],
+        scratch_shapes=[pltpu.VMEM(a.shape, BF) for a in (q, do, osv, q)]
+        + [pltpu.SemaphoreType.DMA((n,)) for n in (15, 15, 12, 12, 16, 16, 3, 8)],
         compiler_params=pltpu.CompilerParams(
             collective_id=0, has_side_effects=True, vmem_limit_bytes=50 * 2**20
         ),
@@ -261,8 +283,8 @@
     return out
 
 
-def reduce_kernel(part_ref, own_ref, hid_ref, rows_ref, cols_ref, hall_ref,
-                  got0, acc0, got1, fwd, acc1, keep1, got2, acc2, colbuf, gotr, gotc,
+def reduce_kernel(part_ref, own_ref, hid_ref, rows_ref, left_ref, hall_ref,
+                  cols_ref, got0, acc0, got1, fwd, acc1, keep1, got2, acc2, colbuf, gotr, gotc,
                   s0, r0, s1, r1, s2, r2, s3, r3, s3c, r3c, s4, r4, s4c, r4c, sh, rh, sp, rp, lsem):
     core, x, yhi, ylo, z = place()
     y = yhi * 2 + ylo
@@ -286,14 +308,11 @@
     opp, right, left = lax.rem(x + 2, 4), lax.rem(x + 1, 4), lax.rem(x + 3, 4)
     chunks = (opp, right, left, x)
 
-    def swap_copy(c, n):
-        return send(part_ref.at[:, 1 - c, :, chunks[n]], got0.at[n], s0.at[n], r0.at[n], partner)
-
-    for c in (0, 1):
-        @pl.when(core == c)
-        def _():
-            for n in range(4):
-                swap_copy(c, n).start()
+    def swap_copy(n):
+        return send(part_ref.at[:, :, chunks[n]], got0.at[n], s0.at[n], r0.at[n], partner)
+
+    for n in range(4):
+        swap_copy(n).start()
     own_hidden = pltpu.make_async_copy(hid_ref, hall_ref.at[core, :, g], lsem)
     own_hidden.start()
     hidden = []
@@ -302,7 +321,7 @@
         copy.start()
         hidden.append(copy)
     def paired(n, py):
-        return total(own_ref[:, core, py, chunks[n]], got0[n, :, py])
+        return total(own_ref[:, py, chunks[n]], got0[n, :, py])
 
     def line_copy(n, src, dst, dx):
         return send(src, dst, s1.at[n], r1.at[n], head_at(0, dx)[1])
@@ -315,18 +334,18 @@
         line_copy(4, acc0.at[0, 0], fwd.at[0], 1),
         line_copy(5, acc0.at[0, 1], fwd.at[1], 3),
     ]
-    swap_copy(0, 0).wait_recv()
+    swap_copy(0).wait_recv()
     acc0[0, 0] = paired(0, 0).astype(BF)
     line[4].start()
     acc0[0, 1] = paired(0, 1).astype(BF)
     line[5].start()
-    swap_copy(0, 1).wait_recv()
+    swap_copy(1).wait_recv()
     acc0[1, 1] = paired(1, 1).astype(BF)
     line[1].start()
-    swap_copy(0, 2).wait_recv()
+    swap_copy(2).wait_recv()
     acc0[2, 0] = paired(2, 0).astype(BF)
     line[2].start()
-    swap_copy(0, 3).wait_recv()
+    swap_copy(3).wait_recv()
     for py in range(2):
         keep1[py] = paired(3, py)
     line[4].wait_recv()
@@ -345,10 +364,11 @@
     summed = total(keep1[yhi], got2[...])
     keep1[0] = summed
     acc2[...] = summed.astype(BF)
-    flat = summed.reshape(64, summed.shape[-1])
-    colbuf[...] = jnp.zeros_like(colbuf)
+    flat = summed.reshape(64, summed.shape[-1]).T
     for k in range(8):
-        colbuf[k, :, 0:72] = flat[:, k * 72:(k + 1) * 72].astype(BF)
+        pair = [flat[k * 72 + n * 36:k * 72 + n * 36 + 36, :] for n in (0, 1)]
+        colbuf[k, 0:36, :] = jnp.concatenate(pair, axis=1).astype(BF)
+        colbuf[k, 36:40, :] = jnp.zeros((4, 128), BF)
     rows, cols = [], []
     for n, d in enumerate(chips):
         to, peer = chip_at(*d)
@@ -381,11 +401,15 @@
     last = send(cols_ref.at[core], cols_ref.at[core], sp.at[1], rp.at[1], partner)
     last.start()
     for n in range(4):
-        swap_copy(0, n).wait_send()
+        swap_copy(n).wait_send()
     for copy in hidden + line + [other] + rows + cols + spread:
         copy.wait_send()
     swap.wait()
     last.wait()
+    for n in range(0, 16, 2):
+        both = [cols_ref[m // 8, m % 8].astype(F32) for m in (n, n + 1)]
+        here = [jnp.where(core == 0, b[:, 0:64], b[:, 64:128]) for b in both]
+        left_ref[:, n * 64:n * 64 + 128] = jnp.concatenate(here, axis=1).astype(BF)
 
 
 def reduce_and_spread(part, own, hidden):
@@ -395,12 +419,13 @@
         reduce_kernel,
         out_shape=[
             jax.ShapeDtypeStruct((8, 8, width), BF),
-            jax.ShapeDtypeStruct((2, 8, 64, 128), BF),
+            jax.ShapeDtypeStruct((40, 1024), BF),
             jax.ShapeDtypeStruct((2, 8, 8, 8, columns), BF),
         ],
         in_specs=[pl.BlockSpec(memory_space=pltpu.VMEM)] * 3,
         out_specs=[pl.BlockSpec(memory_space=pltpu.VMEM)] * 3,
         scratch_shapes=[
+            pltpu.VMEM((2, 8, 40, 128), BF),
             pltpu.VMEM((4, 8, 2, 8, width), BF),
             pltpu.VMEM((3, 2, 8, 8, width), BF),
             pltpu.VMEM((2, 2, 8, 8, width), BF),
@@ -409,9 +434,9 @@
             pltpu.VMEM((2, 8, 8, width), F32),
             pltpu.VMEM((8, 8, width), BF),
             pltpu.VMEM((8, 8, width), BF),
-            pltpu.VMEM((8, 64, 128), BF),
+            pltpu.VMEM((8, 40, 128), BF),
             pltpu.VMEM((7, 8, width), BF),
-            pltpu.VMEM((7, 64, 128), BF),
+            pltpu.VMEM((7, 40, 128), BF),
             dma((4,)), dma((4,)), dma((6,)), dma((6,)), dma, dma, dma((7,)), dma((7,)), dma((7,)), dma((7,)),
             dma((7,)), dma((7,)), dma((7,)), dma((7,)), dma((7,)), dma((7,)), dma((2,)), dma((2,)), dma,
         ],
@@ -431,14 +456,12 @@
     query_grad, part, own = core_attn(
         parents, qt, do, delta, logsumexp.T, keys.reshape(-1, width)
     )
-    shape = (8, 2, 2, 4, 8, width)
+    shape = (8, 2, 4, 8, width)
     row_block, cols, hidden_all = reduce_and_spread(
         part.reshape(shape), own.reshape(shape), hidden.reshape(8, 8, -1)
     )
-    core = lax.rem(lax.axis_index("ba"), 2)
-    cols = lax.dynamic_slice_in_dim(cols.reshape(1024, 128), core * 36, 36, axis=1)
-    weight_grad = lax.dot_general(
-        cols, hidden_all.reshape(1024, -1), (((0,), (0,)), ((), ())), preferred_element_type=F32
+    weight_grad = jnp.dot(
+        cols[:36], hidden_all.reshape(1024, -1), preferred_element_type=F32
     ).astype(BF)
     input_grad = jnp.dot(
         row_block.reshape(64, width), latent_weight, preferred_element_type=F32

time: 77.9 us -> 73.5 us (0.944); the launches traced: 77.1 us -> 73.5 us
  Pallas kernels: 71.7 us -> 70 us
  local copies, waits for them, and re-layouts: 2.46 us -> 0.8 us
    unnamed x12 -> x10, local copies, waits for them, and re-layouts: 2.46 us -> 0.8 us
    pallas_call x1, Pallas kernels: 22.2 us -> 20.8 us  [gather(): pl.pallas_call(gather_kernel, out_shape=[jax.ShapeDtypeStruct((2, 4, 2, 2...]
    pallas_call x1, Pallas kernels: 35.7 us -> 34.7 us  [reduce_and_spread(): pl.pallas_call(reduce_kernel, out_shape=[jax.ShapeDtypeStruct((8, 8, widt...]
where the time goes in v4:
time: 73.5 us
  Pallas kernels  70 us (95%)
  matrix products  2 us (3%)
  local copies, waits for them, and re-layouts  0.8 us (1%)
    pallas_call x1, Pallas kernels, reduce_and_spread(): pl.pallas_call(reduce_kernel, out_shape=[jax.ShapeDtypeStruct((8, 8, widt...  34.7 us
    pallas_call x1, Pallas kernels, gather(): pl.pallas_call(gather_kernel, out_shape=[jax.ShapeDtypeStruct((2, 4, 2, 2...  20.8 us
    pallas_call x1, Pallas kernels, core_attn(): pl.pallas_call(attn_kernel, in_specs=[pl.BlockSpec(memory_space=pltpu.SME...  14.6 us

profile of v4, /device:TPU:1, one launch (start us, length us, event | category | flops | bytes accessed | tf_op | source)
XLA Modules:
  0.0 73.5 jit_solution(2717329371088533271)
XLA Ops:
  0.6 0.0 copy-start
  0.6 0.0 copy-start.2
  0.7 0.8 %copy-done.2 = bf16[8,576]{1,0:T(8,128)(2,1)S(1)} copy-done((bf16[8,576]{1,0:T(8,128)(2,1)S(1)}, bf16[8,576]{1,0:T(8,128)(2,1)}, u32[]{:S(2)}) %copy-start.2) | copy-done | bytes 9240
  1.4 0.0 copy-start.3
  1.4 0.0 copy-start.4
  1.4 20.8 %shard_map.103 = (bf16[2,4,2,2,4,8,576]{6,5,4,3,2,1,0:T(8,128)(2,1)S(1)}, bf16[8,576,256]{2,1,0:T(8,128)(2,1)}, bf16[8,256,512]{2,1,0:T(8,128)(2,1)S(1)}, f32[8,256]{1,0:T(8,128)S(1)}) custom-call(bf16[8,576]{1,0:T(8,128)(2,1)S(1)} %copy-done.2, bf16[8,576,256]{2,1,0:T(8,128)(2,1)} %bitcast.21, bf16[2048,512]{1,0:T(8,128)(2,1)} %bitcast.22, ...), custom_call_target="tpu_custom_call" | custom-call | tf_op jit(solution)/shard_map/pallas_call | solution.py:261
  22.2 0.0 copy-done.3
  22.2 0.0 copy-done.4
  22.2 0.0 copy-start.1
  22.3 14.6 %shard_map.104 = (bf16[8,576,256]{2,1,0:T(8,128)(2,1)}, bf16[8,64,576]{2,1,0:T(8,128)(2,1)S(1)}, f32[8,64,576]{2,1,0:T(8,128)S(1)}) custom-call(s32[256]{0:T(256)S(1)} %copy-done.4, bf16[8,576,256]{2,1,0:T(8,128)(2,1)} %get-tuple-element.13.qt_hbm, bf16[8,256,512]{2,1,0:T(8,128)(2,1)S(1)} %get-tuple-element.14.do_ref, ...), custom_call_target="tpu_custom_call" | custom-call | tf_op jit(solution)/shard_map/pallas_call | solution.py:95
  36.8 0.0 copy-done.1
  36.8 34.7 %shard_map.105 = (bf16[8,8,576]{2,1,0:T(8,128)(2,1)S(1)}, bf16[40,1024]{1,0:T(8,128)(2,1)S(1)}, bf16[2,8,8,8,896]{4,3,2,1,0:T(8,128)(2,1)S(1)}) custom-call(bf16[8,2,4,8,576]{4,3,2,1,0:T(8,128)(2,1)S(1)} %bitcast.18, f32[8,2,4,8,576]{4,3,2,1,0:T(8,128)S(1)} %bitcast.16, bf16[8,8,896]{2,1,0:T(8,128)(2,1)S(1)} %bitcast.19), custom_call_target="tpu_custom_call" | custom-call | tf_op jit(solution)/shard_map/pallas_call | solution.py:418
  71.5 1.0 %convolution_convert_fusion.1 = bf16[36,896]{1,0:T(8,128)(2,1)} fusion(bf16[1024,896]{1,0:T(8,128)(2,1)S(1)} %bitcast.15, bf16[40,1024]{1,0:T(8,128)(2,1)S(1)} %get-tuple-element.20), kind=kOutput, calls=%fused_computation.1 | convolution fusion | flops 66092544 | bytes 1981440 | tf_op jit(solution)/shard_map/dot_general | solution.py:463
  72.6 0.0 copy-done
  72.6 1.0 %convolution_convert_fusion = bf16[64,896]{1,0:T(8,128)(2,1)} fusion(bf16[576,896]{1,0:T(8,128)(2,1)S(1)} %copy-done, bf16[8,8,576]{2,1,0:T(8,128)(2,1)S(1)} %get-tuple-element.22), kind=kOutput, calls=%fused_computation | convolution fusion | flops 66117632 | bytes 1220608 | tf_op jit(solution)/shard_map/dot_general | solution.py:466
Async XLA Ops:
  0.6 71.9 %copy-start = (bf16[576,896]{1,0:T(8,128)(2,1)S(1)}, bf16[576,896]{1,0:T(8,128)(2,1)}, u32[]{:S(2)}) copy-start(bf16[576,896]{1,0:T(8,128)(2,1)} %param.15) | copy-start | bytes 3096580
  0.6 0.8 %copy-start.2 = (bf16[8,576]{1,0:T(8,128)(2,1)S(1)}, bf16[8,576]{1,0:T(8,128)(2,1)}, u32[]{:S(2)}) copy-start(bf16[8,576]{1,0:T(8,128)(2,1)} %lat_ref.1) | copy-start | bytes 27652
  1.4 20.8 %copy-start.3 = (f32[256,8]{0,1:T(8,128)S(1)}, f32[256,8]{0,1:T(8,128)}, u32[]{:S(2)}) copy-start(f32[256,8]{0,1:T(8,128)} %param.11) | copy-start | bytes 24580
  1.4 20.8 %copy-start.4 = (s32[256]{0:T(256)S(1)}, s32[256]{0:T(256)}, u32[]{:S(2)}) copy-start(s32[256]{0:T(256)} %par_ref.1) | copy-start | bytes 3076
  22.2 14.6 %copy-start.1 = (bf16[64,896]{1,0:T(8,128)(2,1)S(1)}, bf16[64,896]{1,0:T(8,128)(2,1)}, u32[]{:S(2)}) copy-start(bf16[64,896]{1,0:T(8,128)(2,1)} %param.14) | copy-start | bytes 344068
